TPU v7x, 32 devices: a whole 2x2x4 slice. The times are simulated.
32 devices in a mesh: rep: 1, dp: 32 (over x, y, z, core).
Axes of the slice: x: 2, y: 2, z: 4, core: 2. Of those that a mesh axis runs over, the one named last changes fastest.
Arguments:
- x: bfloat16 [32, 2048, 768], P(('rep', 'dp'))
- dy: bfloat16 [32, 2048, 768], P(('rep', 'dp'))
- w_gate: bfloat16 [2, 768, 6144], replicated
- w_up: bfloat16 [2, 768, 6144], replicated
- w_down: bfloat16 [2, 6144, 768], replicated
- m_w_gate: float32 [2, 768, 6144], P(None, 'dp')
- m_w_up: float32 [2, 768, 6144], P(None, 'dp')
- m_w_down: float32 [2, 6144, 768], P(None, 'dp')
- v_w_gate: float32 [2, 768, 6144], P(None, 'dp')
- v_w_up: float32 [2, 768, 6144], P(None, 'dp')
- v_w_down: float32 [2, 6144, 768], P(None, 'dp')
Outputs:
- output 1: bfloat16 [2, 768, 6144], P('rep')
- output 2: bfloat16 [2, 768, 6144], P('rep')
- output 3: bfloat16 [2, 6144, 768], P('rep')
- output 4: float32 [2, 768, 6144], P('rep', 'dp')
- output 5: float32 [2, 768, 6144], P('rep', 'dp')
- output 6: float32 [2, 6144, 768], P('rep', 'dp')
- output 7: float32 [2, 768, 6144], P('rep', 'dp')
- output 8: float32 [2, 768, 6144], P('rep', 'dp')
- output 9: float32 [2, 6144, 768], P('rep', 'dp')
All inputs are finite; a program needn't handle non-finite values.
Results may differ from a plain program's by a relative error of at most 0.022.
Values are sent between devices in bfloat16 or wider.
A program may use at most 2 GiB of HBM per device.

v0:
```python
import jax
import jax.numpy as jnp
from jax import lax

NAMES = ("w_gate", "w_up", "w_down")


def matmul(a, w):
    return jnp.dot(a, w, preferred_element_type=jnp.float32).astype(jnp.bfloat16)


def normed(h):
    wide = h.astype(jnp.float32)
    scale = lax.rsqrt(jnp.mean(wide**2, -1, keepdims=True) + 1e-6)
    return (wide * scale).astype(jnp.bfloat16)


def layer(h, w):
    a = normed(h)
    gate = jnp.dot(a, w["w_gate"], preferred_element_type=jnp.float32)
    up = jnp.dot(a, w["w_up"], preferred_element_type=jnp.float32)
    return h + matmul((jax.nn.silu(gate) * up).astype(jnp.bfloat16), w["w_down"])


def adamw(w, m, v, g):
    m = 0.9 * m + 0.1 * g
    v = 0.95 * v + 0.05 * g * g
    step = m * lax.rsqrt(v + 1e-8) + 0.1 * w
    return (w - 0.02 * step).astype(jnp.bfloat16), m, v


def stack(weights, h):
    for number in range(weights["w_gate"].shape[0]):
        h = layer(h, {name: w[number] for name, w in weights.items()})
    return h


def solution(mesh):
    groups = mesh.shape["rep"]

    def step(x, dy, *arrays):
        weights, m, v = (arrays[i : i + 3] for i in (0, 3, 6))
        x, dy = (t.reshape(groups, -1, *t.shape[1:]) for t in (x, dy))

        def of_a_group(x, dy):
            _, back = jax.vjp(lambda w: stack(w, x), dict(zip(NAMES, weights, strict=True)))
            by_weights = back(dy)[0]
            gradients = [by_weights[name].astype(jnp.float32) for name in NAMES]
            new = [adamw(w.astype(jnp.float32), m, v, g) for w, m, v, g in zip(weights, m, v, gradients, strict=True)]
            return tuple(one[which] for which in range(3) for one in new)

        return tuple(t.reshape(-1, *t.shape[2:]) for t in jax.vmap(of_a_group)(x, dy))

    return step
```

profile of v0, /device:TPU:0, one launch (start us, length us, event | category | flops | bytes accessed | tf_op | source)
XLA Modules:
  0.0 2902.8 jit_solution(11763418748650492609)
XLA Ops:
  11.9 30.1 %fusion.170 = f32[2048,6144]{1,0:T(8,128)} fusion(bf16[2,768,6144]{2,1,0:T(8,128)(2,1)} %param.12, bf16[1,2048,768]{1,2,0:T(8,128)(2,1)S(1)} %fusion.183), kind=kOutput, calls=%fused_computation.214 | convolution fusion | flops 19327352832 | bytes 62914560 | tf_op jit(solution)/vmap(jvp())/dot_general | solution.py:20
  42.0 52.9 %fusion.154 = (bf16[1,2048,6144]{2,1,0:T(8,128)(2,1)}, f32[2048,6144]{1,0:T(8,128)}) fusion(f32[2048,6144]{1,0:T(8,128)} %fusion.170, bf16[2,768,6144]{2,1,0:T(8,128)(2,1)} %param.17, bf16[1,2048,768]{1,2,0:T(8,128)(2,1)S(1)} %fusion.183), kind=kOutput, calls=%fused_computation.189 | convolution fusion | flops 19402850304 | bytes 138412032 | tf_op jit(solution)/vmap(jvp())/dot_general | solution.py:21
  94.9 27.4 fusion.186
  125.7 30.1 %fusion.163 = f32[2048,6144]{1,0:T(8,128)} fusion(bf16[2,768,6144]{2,1,0:T(8,128)(2,1)} %param.17, bf16[1,2048,768]{1,2,0:T(8,128)(2,1)S(1)} %fusion.187), kind=kOutput, calls=%fused_computation.207 | convolution fusion | flops 19327352832 | bytes 62914560 | tf_op jit(solution)/vmap(jvp())/dot_general | solution.py:21
  155.8 26.9 convolution_convert_fusion.1
  182.7 71.6 %fusion.143 = (bf16[1,2048,6144]{2,1,0:T(8,128)(2,1)}, bf16[1,2048,6144]{2,1,0:T(8,128)(2,1)}, f32[2048,6144]{1,0:T(8,128)}) fusion(f32[2048,6144]{1,0:T(8,128)} %fusion.163, bf16[2048,6144]{1,0:T(8,128)(2,1)} %convolution_convert_fusion.1, bf16[2,768,6144]{2,1,0:T(8,128)(2,1)} %param.12, bf16[1,2048,768]{1,2,0:T(8,128)(2,1)S(1)} %fusion.187), kind=kOutput, calls=%fused_computation.173 | convolution fusion | flops 19516096512 | bytes 188743680 | tf_op jit(solution)/vmap(jvp())/dot_general | solution.py:20
  254.2 40.1 %fusion.153 = bf16[1,2048,6144]{2,1,0:T(8,128)(2,1)} fusion(f32[2048,6144]{1,0:T(8,128)} %fusion.163, f32[2048,6144]{1,0:T(8,128)} %get-tuple-element.267), kind=kLoop, calls=%fused_computation.187 | loop fusion | flops 75497472 | bytes 125829120 | tf_op jit(solution)/vmap(jvp())/convert_element_type | solution.py:22
  294.4 32.9 %copy.3 = bf16[1,2048,6144]{1,2,0:T(8,128)(2,1)} copy(bf16[1,2048,6144]{2,1,0:T(8,128)(2,1)} %fusion.153) | data formatting | bytes 50331648
  327.3 354.0 %while.16 = (bf16[1,2048,6144]{1,2,0:T(8,128)(2,1)}, bf16[1,2048,768]{2,1,0:T(8,128)(2,1)S(1)}, f32[192,768]{1,0:T(8,128)}, f32[192,768]{1,0:T(8,128)}, u32[]{:T...) while((bf16[1,2048,6144]{1,2,0:T(8,128)(2,1)}, ...), condition=%wide.windowed_dot_general_cond_rs.4.clone, body=%wide.windowed_dot_general_body_rs.4.clone.sunk | while | flops 2423095296 | bytes 77857352 | solution.py:9
  684.3 32.7 %copy.5 = bf16[1,2048,6144]{1,2,0:T(8,128)(2,1)} copy(bf16[1,2048,6144]{2,1,0:T(8,128)(2,1)} %get-tuple-element.263) | data formatting | bytes 50331648
  717.1 25.9 fusion.194
  743.0 27.1 fusion.188
  778.7 364.2 %while.17 = (bf16[1,2048,768]{2,1,0:T(8,128)(2,1)}, bf16[1,2048,6144]{1,2,0:T(8,128)(2,1)}, f32[768,192]{0,1:T(8,128)}, f32[768,192]{0,1:T(8,128)}, u32[]{:T(128...) while((bf16[1,2048,768]{2,1,0:T(8,128)(2,1)}, ...), condition=%wide.windowed_dot_general_cond_rs.5.clone, body=%wide.windowed_dot_general_body_rs.5.clone.sunk | while | flops 2423095296 | bytes 77857352 | solution.py:9
  1142.9 347.5 %while.14 = (bf16[1,2048,6144]{2,1,0:T(8,128)(2,1)}, bf16[1,2048,768]{1,2,0:T(8,128)(2,1)S(1)}, f32[6144,24]{0,1:T(8,128)}, f32[6144,24]{0,1:T(8,128)}, u32[]{:T...) while((bf16[1,2048,6144]{2,1,0:T(8,128)(2,1)}, ...), condition=%wide.windowed_dot_general_cond_rs.2.clone, body=%wide.windowed_dot_general_body_rs.2.clone.sunk | while | flops 2417590272 | bytes 77857352 | solution.py:21
  1150.2 11.4 fusion.321
  1176.7 11.4 fusion.323
  1219.5 11.4 fusion.323
  1262.3 11.4 fusion.323
  1305.1 11.4 fusion.323
  1371.2 11.4 fusion.321
  1390.7 11.4 fusion.323
  1414.0 11.4 fusion.321
  1456.8 11.4 fusion.321
  1490.4 64.3 %convert_multiply_fusion = (bf16[1,2048,6144]{2,1,0:T(8,128)(2,1)}, bf16[1,2048,6144]{2,1,0:T(8,128)(2,1)}) fusion(f32[2048,6144]{1,0:T(8,128)} %fusion.170, f32[2048,6144]{1,0:T(8,128)} %get-tuple-element.264, bf16[2,6144,768]{2,1,0:T(8,128)(2,1)} %param.15, bf16[1,2048,768]{1,2,0:T(8,128)(2,1)} %copy-done.8), kind=kOutput, calls=%fused_computation.168 | convolution fusion | flops 19528679424 | bytes 163577856 | tf_op jit(solution)/vmap(transpose(jvp()))/dot_general | solution.py:9
  1554.7 341.2 %while.15 = (bf16[1,2048,6144]{2,1,0:T(8,128)(2,1)}, bf16[1,2048,768]{1,2,0:T(8,128)(2,1)S(1)}, f32[6144,24]{0,1:T(8,128)}, f32[6144,24]{0,1:T(8,128)}, u32[]{:T...) while((bf16[1,2048,6144]{2,1,0:T(8,128)(2,1)}, ...), condition=%wide.windowed_dot_general_cond_rs.3.clone, body=%wide.windowed_dot_general_body_rs.3.clone.sunk | while | flops 2417590272 | bytes 77857352 | solution.py:21
  1561.8 11.4 fusion.329
  1625.0 11.4 fusion.331
  1710.6 11.4 fusion.331
  1733.9 11.4 fusion.329
  1796.2 11.4 fusion.331
  1881.8 11.4 fusion.331
  1902.1 416.2 %while.12 = (bf16[1,2048,6144]{2,1,0:T(8,128)(2,1)}, bf16[1,2048,768]{1,2,0:T(8,128)(2,1)}, f32[6144,24]{0,1:T(8,128)}, f32[6144,24]{0,1:T(8,128)}, u32[]{:T(128...) while((bf16[1,2048,6144]{2,1,0:T(8,128)(2,1)}, ...), condition=%wide.windowed_dot_general_cond_rs.clone, body=%wide.windowed_dot_general_body_rs.clone.sunk | while | flops 2417590272 | bytes 90440296 | solution.py:20
  1909.4 13.6 fusion.305
  1931.3 11.4 fusion.307
  1963.4 13.6 fusion.305
  1995.3 11.4 fusion.307
  2006.8 11.9 collective-permute-done.3
  2023.3 12.2 collective-permute-start
  2037.4 13.6 fusion.305
  2051.1 11.8 collective-permute-done.1
  2075.5 11.4 fusion.307
  2100.6 13.6 fusion.305
  2122.4 11.4 fusion.307
  2146.7 13.6 fusion.305
  2168.5 11.4 fusion.307
  2191.9 13.6 fusion.305
  2213.7 11.4 fusion.307
  2237.1 13.6 fusion.305
  2258.9 11.4 fusion.307
  2282.3 13.6 fusion.305
  2304.1 11.4 fusion.307
  2324.5 396.3 %while.13 = (bf16[1,2048,6144]{2,1,0:T(8,128)(2,1)}, bf16[1,2048,768]{1,2,0:T(8,128)(2,1)S(1)}, f32[6144,24]{0,1:T(8,128)}, f32[6144,24]{0,1:T(8,128)}, u32[]{:T...) while((bf16[1,2048,6144]{2,1,0:T(8,128)(2,1)}, ...), condition=%wide.windowed_dot_general_cond_rs.1.clone, body=%wide.windowed_dot_general_body_rs.1.clone.sunk | while | flops 2417590272 | bytes 77857352 | solution.py:20
  2331.6 11.4 fusion.313
  2392.7 12.9 collective-permute-done.4
  2475.7 11.9 collective-permute-start.6
  2487.6 11.4 fusion.315
  2533.2 11.4 fusion.315
  2556.5 11.4 fusion.313
  2576.0 11.4 fusion.315
  2621.0 11.4 fusion.315
  2706.6 11.4 fusion.315
  2722.2 11.4 collective-permute-done.25
  2738.2 119.7 %all-gather.10.cloned.1.call-done = bf16[1,2,768,6144]{3,2,1,0:T(8,128)(2,1)} async-done(((bf16[1,2,24,6144]{3,2,1,0:T(8,128)(2,1)}), bf16[1,2,768,6144]{3,2,1,0:T(8,128)(2,1)}) %all-gather.10.cloned.1.call-update) | async-done | bytes 18874384 | tf_op jit(solution)/reshape | solution.py:52
  2857.8 20.5 copy.63
  (747 shorter events, 1762.0 us)
Async XLA Ops:
  7.2 2731.0 %all-gather.14.cloned.1.call-start = ((), (), s32[]{:S(2)}) async-start(), calls=%async_computation.2 | async-start | bytes 19464192 | tf_op jit(solution)/reshape | solution.py:52
  386.0 18.9 collective-permute-start.18
  429.5 18.9 collective-permute-start.18
  429.5 18.9 collective-permute-start.19
  614.0 18.7 collective-permute-start.18
  614.0 18.7 collective-permute-start.19
  660.1 18.7 collective-permute-start.18
  660.1 18.7 collective-permute-start.19
  681.3 1214.7 %collective-permute-start.28 = (f32[192,768]{1,0:T(8,128)}, f32[192,768]{1,0:T(8,128)}, u32[]{:S(2)}, u32[]{:S(2)}) collective-permute-start(f32[192,768]{1,0:T(8,128)} %get-tuple-element.45), channel_id=32, source_target_pairs={{0,1},{1,2},{2,3},{3,4},{4,5},{5,6},{6,7},{7,8},{8,9},{9,10},{10,1... | collective-permute-start | bytes 1769480 | tf_op jit(solution)/vmap(transpose(jvp()))/dot_general | solution.py:9
  801.5 18.7 collective-permute-start.22
  801.5 18.7 collective-permute-start.23
  847.2 18.7 collective-permute-start.22
  847.2 18.7 collective-permute-start.23
  893.0 18.7 collective-permute-start.22
  893.0 18.7 collective-permute-start.23
  938.7 18.7 collective-permute-start.22
  938.7 18.7 collective-permute-start.23
  984.5 18.7 collective-permute-start.22
  984.5 18.7 collective-permute-start.23
  1030.2 18.7 collective-permute-start.22
  1030.2 18.7 collective-permute-start.23
  1121.7 18.7 collective-permute-start.23
  1142.9 754.5 %collective-permute-start.29 = (f32[768,192]{0,1:T(8,128)}, f32[768,192]{0,1:T(8,128)}, u32[]{:S(2)}, u32[]{:S(2)}) collective-permute-start(f32[768,192]{0,1:T(8,128)} %get-tuple-element.47), channel_id=38, source_target_pairs={{0,1},{1,2},{2,3},{3,4},{4,5},{5,6},{6,7},{7,8},{8,9},{9,10},{10,1... | collective-permute-start | bytes 1769480 | tf_op jit(solution)/vmap(transpose(jvp()))/dot_general | solution.py:9
  1143.8 24.9 collective-permute-start.8
  1144.6 24.0 collective-permute-start.9
  1490.4 827.9 %collective-permute-start.26 = (f32[6144,24]{0,1:T(8,128)}, f32[6144,24]{0,1:T(8,128)}, u32[]{:S(2)}, u32[]{:S(2)}) collective-permute-start(f32[6144,24]{0,1:T(8,128)} %get-tuple-element.41), channel_id=19, source_target_pairs={{0,1},{1,2},{2,3},{3,4},{4,5},{5,6},{6,7},{7,8},{8,9},{9,10},{10,1... | collective-permute-start | bytes 1769480 | tf_op jit(solution)/vmap(transpose(jvp()))/dot_general | solution.py:21
  1895.9 423.9 %collective-permute-start.27 = (f32[6144,24]{0,1:T(8,128)}, f32[6144,24]{0,1:T(8,128)}, u32[]{:S(2)}, u32[]{:S(2)}) collective-permute-start(f32[6144,24]{0,1:T(8,128)} %get-tuple-element.43), channel_id=25, source_target_pairs={{0,1},{1,2},{2,3},{3,4},{4,5},{5,6},{6,7},{7,8},{8,9},{9,10},{10,1... | collective-permute-start | bytes 1769480 | tf_op jit(solution)/vmap(transpose(jvp()))/dot_general | solution.py:21
  1902.1 836.1 %all-gather.12.cloned.1.call-start = ((), (), s32[]{:S(2)}) async-start(), calls=%async_computation.1 | async-start | bytes 19464192 | tf_op jit(solution)/reshape | solution.py:52
  1903.2 19.8 collective-permute-start
  1904.1 19.0 collective-permute-start.1
  1926.0 25.6 collective-permute-start.2
  1926.0 25.6 collective-permute-start.3
  1956.2 31.1 %collective-permute-start = (f32[6144,24]{0,1:T(8,128)}, f32[6144,24]{0,1:T(8,128)}, u32[]{:S(2)}, u32[]{:S(2)}) collective-permute-start(f32[6144,24]{0,1:T(8,128)} %broadcast_select_fusion.24), channel_id=3, source_target_pairs={{0,1},{1,2},{2,3},{3,4},{4,5},{5,6},{6,7},{7,8},{8,9},{9,10},{10,1... | collective-permute-start | bytes 1769480 | tf_op jit(solution)/vmap(transpose(jvp()))/dot_general | solution.py:20
  1958.1 29.2 %collective-permute-start.1 = (f32[6144,24]{0,1:T(8,128)}, f32[6144,24]{0,1:T(8,128)}, u32[]{:S(2)}, u32[]{:S(2)}) collective-permute-start(f32[6144,24]{0,1:T(8,128)} %broadcast_select_fusion.25), channel_id=2, source_target_pairs={{0,31},{1,0},{2,1},{3,2},{4,3},{5,4},{6,5},{7,6},{8,7},{9,8},{10,9... | collective-permute-start | bytes 1769480 | tf_op jit(solution)/vmap(transpose(jvp()))/dot_general | solution.py:20
  1993.8 24.8 collective-permute-start.3
  2023.3 27.8 collective-permute-start
  2037.4 25.5 collective-permute-start.1
  2065.6 21.3 collective-permute-start.2
  2093.1 21.1 collective-permute-start
  2095.0 19.2 collective-permute-start.1
  2139.4 20.9 collective-permute-start
  2141.3 19.0 collective-permute-start.1
  2184.6 20.9 collective-permute-start
  2186.5 19.0 collective-permute-start.1
  2229.8 20.9 collective-permute-start
  2231.7 19.0 collective-permute-start.1
  2275.0 20.9 collective-permute-start
  2276.9 19.0 collective-permute-start.1
  2318.3 402.5 %collective-permute-start.24 = (f32[6144,24]{0,1:T(8,128)}, f32[6144,24]{0,1:T(8,128)}, u32[]{:S(2)}, u32[]{:S(2)}) collective-permute-start(f32[6144,24]{0,1:T(8,128)} %get-tuple-element.37), channel_id=6, source_target_pairs={{0,1},{1,2},{2,3},{3,4},{4,5},{5,6},{6,7},{7,8},{8,9},{9,10},{10,1... | collective-permute-start | bytes 1769480 | tf_op jit(solution)/vmap(transpose(jvp()))/dot_general | solution.py:20
  2324.4 533.4 %all-gather.10.cloned.1.call-start = ((), (), s32[]{:S(2)}) async-start(), calls=%async_computation | async-start | bytes 19464192 | tf_op jit(solution)/reshape | solution.py:52
  2325.4 19.5 collective-permute-start.4
  2326.2 21.7 collective-permute-start.5
  2350.6 18.7 collective-permute-start.6
  2350.6 18.7 collective-permute-start.7
  2374.0 31.5 %collective-permute-start.4 = (f32[6144,24]{0,1:T(8,128)}, f32[6144,24]{0,1:T(8,128)}, u32[]{:S(2)}, u32[]{:S(2)}) collective-permute-start(f32[6144,24]{0,1:T(8,128)} %broadcast_select_fusion.26), channel_id=9, source_target_pairs={{0,1},{1,2},{2,3},{3,4},{4,5},{5,6},{6,7},{7,8},{8,9},{9,10},{10,1... | collective-permute-start | bytes 1769480 | tf_op jit(solution)/vmap(transpose(jvp()))/dot_general | solution.py:20
  2375.9 29.6 %collective-permute-start.5 = (f32[6144,24]{0,1:T(8,128)}, f32[6144,24]{0,1:T(8,128)}, u32[]{:S(2)}, u32[]{:S(2)}) collective-permute-start(f32[6144,24]{0,1:T(8,128)} %broadcast_select_fusion.27), channel_id=8, source_target_pairs={{0,31},{1,0},{2,1},{3,2},{4,3},{5,4},{6,5},{7,6},{8,7},{9,8},{10,9... | collective-permute-start | bytes 1769480 | tf_op jit(solution)/vmap(transpose(jvp()))/dot_general | solution.py:20
  2408.3 20.9 collective-permute-start.6
  2409.5 25.9 collective-permute-start.7
  2440.0 28.9 collective-permute-start.4
  2447.5 25.5 collective-permute-start.5
  2475.7 23.3 collective-permute-start.6
  2505.2 19.9 collective-permute-start.4
  2570.7 19.0 collective-permute-start.6
  2570.7 19.0 collective-permute-start.7
  (169 other events, 3298.0 us)
Sparse Core Ops, SparseCore 0:
  1902.2 171.7 all-gather.13
  2324.6 162.7 all-gather.11
  2738.2 119.5 all-gather.9
where the time goes:
time: 2920 us; the launch traced here: 2900 us
  matrix products  1210 us (41%)
  waiting for transfers between devices  538 us (18%)
  starting transfers between devices  536 us (18%)
  other arithmetic  491 us (17%)
  local copies, waits for them, and re-layouts  114 us (4%)
    dot_general x35, matrix products, layer(): gate = jnp.dot(a, w['w_gate'], preferred_element_type=jnp.float32)  512 us
    dot_general x35, matrix products, layer(): up = jnp.dot(a, w['w_up'], preferred_element_type=jnp.float32)  474 us
    dot_general x66, waiting for transfers between devices, matmul(): jnp.dot(a, w, preferred_element_type=jnp.float32).astype(jnp.bfloat16)  305 us
    dot_general x35, matrix products, matmul(): jnp.dot(a, w, preferred_element_type=jnp.float32).astype(jnp.bfloat16)  222 us
    dot_general x66, starting transfers between devices, layer(): gate = jnp.dot(a, w['w_gate'], preferred_element_type=jnp.float32)  191 us
    dot_general x66, starting transfers between devices, matmul(): jnp.dot(a, w, preferred_element_type=jnp.float32).astype(jnp.bfloat16)  175 us
    dot_general x96, other arithmetic  171 us
    dot_general x66, starting transfers between devices, layer(): up = jnp.dot(a, w['w_up'], preferred_element_type=jnp.float32)  171 us
  transfers between devices with their start and end apart: 201, of which 67 were waited for; matrix products, arithmetic and copies ran while one was open for 48% of the time, Pallas kernels for 0%

commit v1 on v0

v1 whole, which is shorter than its diff:
```python
import jax
import jax.numpy as jnp
from jax import lax
from jax.sharding import PartitionSpec as P

BF = jnp.bfloat16
F32 = jnp.float32


def dot(a, b, dims):
    return lax.dot_general(a, b, (dims, ((), ())), preferred_element_type=F32)


def scale_of(h):
    wide = h.astype(F32)
    return wide, lax.rsqrt(jnp.mean(wide**2, -1, keepdims=True) + 1e-6)


def norm_back(h, da):
    wide, scale = scale_of(h)
    da = da.astype(F32)
    along = jnp.sum(da * wide, -1, keepdims=True)
    return (da * scale - wide * (scale**3 * along / h.shape[-1])).astype(BF)


def gated(gate, up):
    return (jax.nn.silu(gate) * up).astype(BF)


def gated_back(gate, up, dp):
    s = jax.nn.sigmoid(gate)
    dp = dp.astype(F32)
    d_up = dp * (gate * s)
    d_gate = dp * up * (s * (1 + gate * (1 - s)))
    return d_gate.astype(BF), d_up.astype(BF)


def adamw(w, m, v, g):
    g = g.astype(F32)
    w = w.astype(F32)
    m = 0.9 * m + 0.1 * g
    v = 0.95 * v + 0.05 * g * g
    step = m * lax.rsqrt(v + 1e-8) + 0.1 * w
    return (w - 0.02 * step).astype(BF), m, v


NN, NT, TN = ((1,), (0,)), ((1,), (1,)), ((0,), (0,))


def solution(mesh):
    axis = "dp"
    n = mesh.shape["dp"]

    def step(x, dy, *arrays):
        wg, wu, wd = arrays[:3]
        ms, vs = arrays[3:6], arrays[6:9]
        x, dy = x[0], dy[0]
        layers = wg.shape[0]
        me = lax.axis_index(axis)
        new = [[None] * layers for _ in range(3)]

        def update(which, layer, grad):
            g = lax.psum_scatter(grad.astype(BF), axis, scatter_dimension=0, tiled=True)
            w = arrays[which][layer]
            rows = w.shape[0] // n
            mine = lax.dynamic_slice_in_dim(w, me * rows, rows, 0)
            w, m, v = adamw(mine, ms[which][layer], vs[which][layer], g)
            w = lax.all_gather(w, axis, axis=0, tiled=True)
            new[which][layer] = (w, m, v)

        h = x
        saved = []
        for layer in range(layers):
            wide, scale = scale_of(h)
            a = (wide * scale).astype(BF)
            gate, up = dot(a, wg[layer], NN), dot(a, wu[layer], NN)
            p = gated(gate, up)
            saved.append((h, a, gate, up, p))
            if layer < layers - 1:
                h = h + dot(p, wd[layer], NN).astype(BF)
        dh = dy
        for layer in reversed(range(layers)):
            h, a, gate, up, p = saved[layer]
            update(2, layer, dot(p, dh, TN))
            dp = dot(dh, wd[layer], NT).astype(BF)
            d_gate, d_up = gated_back(gate, up, dp)
            update(0, layer, dot(a, d_gate, TN))
            update(1, layer, dot(a, d_up, TN))
            if layer:
                da = dot(d_gate, wg[layer], NT).astype(BF) + dot(d_up, wu[layer], NT).astype(BF)
                dh = dh + norm_back(h, da)
        return tuple(jnp.stack([new[i][layer][k] for layer in range(layers)]) for k in range(3) for i in range(3))

    seq = P(("rep", "dp"))
    whole = P()
    rows = P(None, "dp")
    return jax.shard_map(
        step,
        mesh=mesh,
        in_specs=(seq, seq) + (whole,) * 3 + (rows,) * 6,
        out_specs=(P("rep"),) * 3 + (P("rep", "dp"),) * 6,
        check_vma=False,
    )
```

time: 2920 us -> 1710 us (0.59)
  matrix products: 1210 us -> 505 us
  starting transfers between devices: 536 us -> 0.49 us
  waiting for transfers between devices: 538 us -> 1050 us
  other arithmetic: 491 us -> 71.8 us
  local copies, waits for them, and re-layouts: 114 us -> 53.2 us
    dot_general x105 -> x15, matrix products: 1210 us -> 505 us  [dot(): return lax.dot_general(a, b, (dims, ((), ())), preferred_element_type=F32)]
    reduce_scatter x0 -> x6, waiting for transfers between devices: none -> 594 us  [update(): g = lax.psum_scatter(grad.astype(BF), axis, scatter_dimension=0, tiled=True)]
    dot_general x198 -> x0, starting transfers between devices: 536 us -> none  [the longest x66 191 us: layer(): gate = jnp.dot(a, w['w_gate'], preferred_element_type=jnp.float32)]
    all_gather x0 -> x6, waiting for transfers between devices: none -> 457 us  [update(): w = lax.all_gather(w, axis, axis=0, tiled=True)]
    dot_general x192 -> x0, other arithmetic: 424 us -> none
    dot_general x198 -> x0, waiting for transfers between devices: 418 us -> none  [the longest x66 305 us: matmul(): jnp.dot(a, w, preferred_element_type=jnp.float32).astype(jnp.bfloat16)]
    reshape x3 -> x0, waiting for transfers between devices: 120 us -> none  [step(): t.reshape(-1, *t.shape[2:])]
    unnamed x56 -> x38, local copies, waits for them, and re-layouts: 114 us -> 9.6 us
  transfers between devices with their start and end apart: 201 -> 12, of which waited for: 67 -> 11; matrix products, arithmetic and copies ran while one was open for 48% -> 17% of each run, Pallas kernels for 0% -> 0%
where the time goes in v1:
time: 1710 us; the launch traced here: 1700 us
  waiting for transfers between devices  1050 us (61%)
  matrix products  505 us (30%)
  other arithmetic  71.8 us (4%)
  local copies, waits for them, and re-layouts  53.2 us (3%)
    reduce_scatter x6, waiting for transfers between devices, update(): g = lax.psum_scatter(grad.astype(BF), axis, scatter_dimension=0, tiled=True)  594 us
    dot_general x15, matrix products, dot(): return lax.dot_general(a, b, (dims, ((), ())), preferred_element_type=F32)  505 us
    all_gather x6, waiting for transfers between devices, update(): w = lax.all_gather(w, axis, axis=0, tiled=True)  457 us
    another operation x6, other arithmetic, step(): jnp.stack([new[i][layer][k] for layer in range(layers)])  55.4 us
  transfers between devices with their start and end apart: 12, of which 11 were waited for; matrix products, arithmetic and copies ran while one was open for 17% of the time, Pallas kernels for 0%

profile of v1, /device:TPU:0, one launch (start us, length us, event | category | flops | bytes accessed | tf_op | source)
XLA Modules:
  0.0 1697.3 jit_solution(16110335336026635521)
XLA Ops:
  7.2 0.0 reduce-scatter.15.cloned.1.call-start
  7.2 3.2 copy.20
  10.4 0.7 fusion.38
  11.1 29.5 %fusion.33 = f32[2048,6144]{1,0:T(8,128)} fusion(bf16[1,2048,768]{2,1,0:T(8,128)(2,1)} %param.11, f32[2048]{0:T(1024)S(1)} %add_rsqrt_fusion.1, bf16[2,768,6144]{2,1,0:T(8,128)(2,1)} %param.13), kind=kOutput, calls=%fused_computation.47 | convolution fusion | flops 19332071424 | bytes 62922752 | tf_op jit(solution)/shard_map/dot_general | solution.py:11
  40.7 48.7 %multiply_convert_fusion.1 = (bf16[2048,6144]{1,0:T(8,128)(2,1)}, f32[2048,6144]{1,0:T(8,128)}) fusion(f32[2048,6144]{1,0:T(8,128)} %fusion.33, bf16[2,768,6144]{2,1,0:T(8,128)(2,1)} %param.14, bf16[1,2048,768]{2,1,0:T(8,128)(2,1)} %param.11, f32[2048]{0:T(1024)S(1)} %add_rsqrt_fusion.1), kind=kOutput, calls=%fused_computation.13 | convolution fusion | flops 19407568896 | bytes 138420224 | tf_op jit(solution)/shard_map/dot_general | solution.py:11
  89.4 27.4 %fusion.42 = (f32[2048]{0:T(1024)S(1)}, bf16[2048,768]{0,1:T(8,128)(2,1)}) fusion(bf16[2048,6144]{1,0:T(8,128)(2,1)} %get-tuple-element.35, bf16[2,6144,768]{2,1,0:T(8,128)(2,1)} %param.15, bf16[1,2048,768]{1,2,0:T(8,128)(2,1)S(1)} %copy.20), kind=kOutput, calls=%fused_computation.57 | convolution fusion | flops 19335215104 | bytes 40902656 | tf_op jit(solution)/shard_map/dot_general | solution.py:11
  116.8 29.2 %fusion.26 = f32[2048,6144]{1,0:T(8,128)} fusion(bf16[2048,768]{0,1:T(8,128)(2,1)} %get-tuple-element.38, f32[2048]{0:T(1024)S(1)} %add_rsqrt_fusion, bf16[2,768,6144]{2,1,0:T(8,128)(2,1)} %param.14), kind=kOutput, calls=%fused_computation.40 | convolution fusion | flops 19332071424 | bytes 62922752 | tf_op jit(solution)/shard_map/dot_general | solution.py:11
  146.0 29.2 %fusion.22 = f32[2048,6144]{1,0:T(8,128)} fusion(bf16[2048,768]{0,1:T(8,128)(2,1)S(1)} %copy-done.4, f32[2048]{0:T(1024)S(1)} %add_rsqrt_fusion, bf16[2,768,6144]{2,1,0:T(8,128)(2,1)} %param.13), kind=kOutput, calls=%fused_computation.36 | convolution fusion | flops 19332071424 | bytes 62922752 | tf_op jit(solution)/shard_map/dot_general | solution.py:11
  175.2 2.9 copy.21
  178.1 60.4 %fusion.2 = (bf16[2048,6144]{1,0:T(8,128)(2,1)}, bf16[2048,6144]{1,0:T(8,128)(2,1)}) fusion(f32[2048,6144]{1,0:T(8,128)} %fusion.22, f32[2048,6144]{1,0:T(8,128)} %fusion.26, bf16[2,6144,768]{2,1,0:T(8,128)(2,1)} %param.15, bf16[1,2048,768]{2,1,0:T(8,128)(2,1)S(1)} %copy-done.3), kind=kOutput, calls=%fused_computation.6 | convolution fusion | flops 19516096512 | bytes 163577856 | tf_op jit(solution)/shard_map/dot_general | solution.py:11
  238.4 26.8 %fusion.48 = bf16[2048,768]{0,1:T(8,128)(2,1)} fusion(bf16[2048,6144]{1,0:T(8,128)(2,1)} %get-tuple-element.9, bf16[2,768,6144]{2,1,0:T(8,128)(2,1)} %param.14), kind=kOutput, calls=%fused_computation.62 | convolution fusion | flops 19328925696 | bytes 37748736 | tf_op jit(solution)/shard_map/dot_general | solution.py:11
  265.3 27.9 %fusion.44 = (f32[2048]{0:T(1024)S(1)}, bf16[2048,768]{0,1:T(8,128)(2,1)}) fusion(bf16[2048,768]{0,1:T(8,128)(2,1)} %get-tuple-element.38, bf16[2048,768]{0,1:T(8,128)(2,1)} %fusion.48, bf16[2048,6144]{1,0:T(8,128)(2,1)} %get-tuple-element.10, bf16[2,768,6144]{2,1,0:T(8,128)(2,1)} %param.13), kind=kOutput, calls=%fused_computation.59 | convolution fusion | flops 19336787968 | bytes 44048384 | tf_op jit(solution)/shard_map/dot_general | solution.py:11
  293.2 5.1 fusion.55
  298.3 1.7 copy-done.6
  299.9 26.9 %convolution_convert_fusion.4 = bf16[6144,768]{1,0:T(8,128)(2,1)} fusion(bf16[2048,6144]{1,0:T(8,128)(2,1)} %get-tuple-element.35, bf16[2048,768]{0,1:T(8,128)(2,1)S(1)} %fusion.55), kind=kOutput, calls=%fused_computation.33 | convolution fusion | flops 19332071424 | bytes 37748736 | tf_op jit(solution)/shard_map/dot_general | solution.py:11
  326.9 0.0 reduce-scatter.15.cloned.1.call-update
  326.9 0.0 reduce-scatter.17.cloned.1.call-start
  327.0 42.1 %fusion.16 = bf16[6144,768]{1,0:T(8,128)(2,1)} fusion(f32[2048,6144]{1,0:T(8,128)} %fusion.26, f32[2048,6144]{1,0:T(8,128)} %fusion.22, bf16[1,2048,768]{2,1,0:T(8,128)(2,1)S(1)} %copy-done.3), kind=kOutput, calls=%fused_computation.29 | convolution fusion | flops 19407568896 | bytes 113246208 | tf_op jit(solution)/shard_map/dot_general | solution.py:11
  369.1 0.0 reduce-scatter.17.cloned.1.call-update
  369.1 0.0 reduce-scatter.13.cloned.1.call-start
  369.2 1.8 copy-done.5
  371.0 25.1 %convolution_convert_fusion.2 = bf16[768,6144]{1,0:T(8,128)(2,1)} fusion(bf16[2048,6144]{1,0:T(8,128)(2,1)} %get-tuple-element.9, bf16[2048,768]{0,1:T(8,128)(2,1)S(1)} %copy-done.5, f32[2048]{0:T(1024)S(1)} %copy-done.13), kind=kOutput, calls=%fused_computation.30 | convolution fusion | flops 19336790016 | bytes 37756928 | tf_op jit(solution)/shard_map/dot_general | solution.py:11
  396.1 0.0 reduce-scatter.13.cloned.1.call-update
  396.2 0.0 reduce-scatter.11.cloned.1.call-start
  396.2 26.9 %convolution_convert_fusion = bf16[2048,6144]{1,0:T(8,128)(2,1)} fusion(bf16[2048,768]{0,1:T(8,128)(2,1)} %copy-done.6, bf16[2,6144,768]{2,1,0:T(8,128)(2,1)} %param.15), kind=kOutput, calls=%fused_computation.19 | convolution fusion | flops 19339935744 | bytes 37748736 | tf_op jit(solution)/shard_map/dot_general | solution.py:11
  423.1 32.2 %fusion.17 = bf16[768,6144]{1,0:T(8,128)(2,1)} fusion(bf16[2048,6144]{1,0:T(8,128)(2,1)} %convolution_convert_fusion, f32[2048,6144]{1,0:T(8,128)} %fusion.33, bf16[1,2048,768]{1,2,0:T(8,128)(2,1)S(1)} %copy-done.1, f32[2048]{0:T(1024)S(1)} %copy-done.17), kind=kOutput, calls=%fused_computation.32 | convolution fusion | flops 19424870400 | bytes 88088576 | tf_op jit(solution)/shard_map/dot_general | solution.py:11
  455.3 0.0 reduce-scatter.9.cloned.1.call-start
  455.3 26.1 %convolution_convert_fusion.3 = bf16[768,6144]{1,0:T(8,128)(2,1)} fusion(bf16[2048,6144]{1,0:T(8,128)(2,1)} %get-tuple-element.10, bf16[2048,768]{0,1:T(8,128)(2,1)} %get-tuple-element.38, f32[2048]{0:T(1024)S(1)} %copy-done.13), kind=kOutput, calls=%fused_computation.31 | convolution fusion | flops 19336790016 | bytes 37756928 | tf_op jit(solution)/shard_map/dot_general | solution.py:11
  481.5 0.0 reduce-scatter.7.cloned.1.call-start
  481.5 46.4 %fusion.13 = bf16[768,6144]{1,0:T(8,128)(2,1)} fusion(f32[2048,6144]{1,0:T(8,128)} %get-tuple-element.36, bf16[2048,6144]{1,0:T(8,128)(2,1)} %convolution_convert_fusion, f32[2048,6144]{1,0:T(8,128)} %fusion.33, bf16[1,2048,768]{1,2,0:T(8,128)(2,1)S(1)} %copy-done.1, f32[2048]{0:T(1024)S(1)} %copy-done.17), kind=kOutput, calls=%fused_computation.28 | convolution fusion | flops 19475202048 | bytes 138420224 | tf_op jit(solution)/shard_map/dot_general | solution.py:11
  528.0 0.0 all-gather.15.cloned.1.call-start
  528.0 14.7 fusion.127
  542.7 64.8 %reduce-scatter.17.cloned.1.call-done = bf16[192,768]{1,0:T(8,128)(2,1)} async-done(((bf16[6144,768]{1,0:T(8,128)(2,1)}), bf16[192,768]{1,0:T(8,128)(2,1)}) %reduce-scatter.17.cloned.1.call-update) | async-done | bytes 294928 | tf_op jit(solution)/shard_map/reduce_scatter | solution.py:63
  607.5 3.0 fusion.91
  610.5 0.0 all-gather.17.cloned.1.call-start
  610.6 0.7 all-gather.17.cloned.1.call-update
  611.3 0.0 all-gather.11.cloned.1.call-start
  611.3 14.5 fusion.128
  625.8 122.9 %reduce-scatter.13.cloned.1.call-done = bf16[24,6144]{1,0:T(8,128)(2,1)} async-done(((bf16[768,6144]{1,0:T(8,128)(2,1)}), bf16[24,6144]{1,0:T(8,128)(2,1)}) %reduce-scatter.13.cloned.1.call-update) | async-done | bytes 294928 | tf_op jit(solution)/shard_map/reduce_scatter | solution.py:63
  748.7 141.8 %reduce-scatter.11.cloned.1.call-done = bf16[24,6144]{1,0:T(8,128)(2,1)} async-done(((bf16[768,6144]{1,0:T(8,128)(2,1)}), bf16[24,6144]{1,0:T(8,128)(2,1)}) %reduce-scatter.11.cloned.1.call-update) | async-done | bytes 294928 | tf_op jit(solution)/shard_map/reduce_scatter | solution.py:63
  890.5 3.7 fusion.85
  894.2 0.0 all-gather.11.cloned.1.call-update
  894.2 0.0 all-gather.13.cloned.1.call-start
  894.3 0.5 all-gather.13.cloned.1.call-update
  894.8 0.0 all-gather.7.cloned.1.call-start
  894.8 14.5 fusion.129
  909.3 122.4 %reduce-scatter.9.cloned.1.call-done = bf16[24,6144]{1,0:T(8,128)(2,1)} async-done(((bf16[768,6144]{1,0:T(8,128)(2,1)}), bf16[24,6144]{1,0:T(8,128)(2,1)}) %reduce-scatter.9.cloned.1.call-update) | async-done | bytes 294928 | tf_op jit(solution)/shard_map/reduce_scatter | solution.py:63
  1031.7 141.7 %reduce-scatter.7.cloned.1.call-done = bf16[24,6144]{1,0:T(8,128)(2,1)} async-done(((bf16[768,6144]{1,0:T(8,128)(2,1)}), bf16[24,6144]{1,0:T(8,128)(2,1)}) %reduce-scatter.7.cloned.1.call-update) | async-done | bytes 294928 | tf_op jit(solution)/shard_map/reduce_scatter | solution.py:63
  1173.4 3.8 fusion.79
  1177.2 0.0 all-gather.7.cloned.1.call-update
  1177.2 0.0 all-gather.9.cloned.1.call-start
  1177.3 0.5 all-gather.9.cloned.1.call-update
  1177.9 1.6 pad_maximum_fusion.5
  1179.4 2.8 pad_maximum_fusion.4
  1182.2 1.6 pad_maximum_fusion.3
  1183.8 73.2 %all-gather.15.cloned.1.call-done = bf16[6144,768]{1,0:T(8,128)(2,1)} async-done(((bf16[192,768]{1,0:T(8,128)(2,1)}), bf16[6144,768]{1,0:T(8,128)(2,1)}) %all-gather.15.cloned.1.call-update) | async-done | bytes 9437200 | tf_op jit(solution)/shard_map/all_gather | solution.py:68
  1256.9 83.4 %all-gather.17.cloned.1.call-done = bf16[6144,768]{1,0:T(8,128)(2,1)} async-done(((bf16[192,768]{1,0:T(8,128)(2,1)}), bf16[6144,768]{1,0:T(8,128)(2,1)}) %all-gather.17.cloned.1.call-update) | async-done | bytes 9437200 | tf_op jit(solution)/shard_map/all_gather | solution.py:68
  1340.3 16.6 pad_maximum_fusion.2
  1356.9 66.8 %all-gather.11.cloned.1.call-done = bf16[768,6144]{1,0:T(8,128)(2,1)} async-done(((bf16[24,6144]{1,0:T(8,128)(2,1)}), bf16[768,6144]{1,0:T(8,128)(2,1)}) %all-gather.11.cloned.1.call-update) | async-done | bytes 9437200 | tf_op jit(solution)/shard_map/all_gather | solution.py:68
  1423.7 83.2 %all-gather.13.cloned.1.call-done = bf16[768,6144]{1,0:T(8,128)(2,1)} async-done(((bf16[24,6144]{1,0:T(8,128)(2,1)}), bf16[768,6144]{1,0:T(8,128)(2,1)}) %all-gather.13.cloned.1.call-update) | async-done | bytes 9437200 | tf_op jit(solution)/shard_map/all_gather | solution.py:68
  1506.9 16.5 pad_maximum_fusion.1
  1523.4 66.9 %all-gather.7.cloned.1.call-done = bf16[768,6144]{1,0:T(8,128)(2,1)} async-done(((bf16[24,6144]{1,0:T(8,128)(2,1)}), bf16[768,6144]{1,0:T(8,128)(2,1)}) %all-gather.7.cloned.1.call-update) | async-done | bytes 9437200 | tf_op jit(solution)/shard_map/all_gather | solution.py:68
  1590.3 83.2 %all-gather.9.cloned.1.call-done = bf16[768,6144]{1,0:T(8,128)(2,1)} async-done(((bf16[24,6144]{1,0:T(8,128)(2,1)}), bf16[768,6144]{1,0:T(8,128)(2,1)}) %all-gather.9.cloned.1.call-update) | async-done | bytes 9437200 | tf_op jit(solution)/shard_map/all_gather | solution.py:68
  1673.5 16.5 pad_maximum_fusion
  (42 shorter events, 0.2 us)
Async XLA Ops:
  7.2 535.5 %reduce-scatter.15.cloned.1.call-start = ((), (), s32[]{:S(2)}) async-start(), calls=%async_computation.14 | async-start | bytes 9732096 | tf_op jit(solution)/shard_map/reduce_scatter | solution.py:63
  10.4 78.9 %copy-start = (bf16[1,2048,768]{1,2,0:T(8,128)(2,1)}, bf16[1,2048,768]{1,2,0:T(8,128)(2,1)S(1)}, u32[]{:S(2)}) copy-start(bf16[1,2048,768]{1,2,0:T(8,128)(2,1)S(1)} %copy.20) | copy-start | bytes 9437188
  11.1 29.6 %copy-start.16 = (f32[2048]{0:T(1024)}, f32[2048]{0:T(1024)S(1)}, u32[]{:S(2)}) copy-start(f32[2048]{0:T(1024)S(1)} %add_rsqrt_fusion.1) | copy-start | bytes 24580
  116.8 29.2 %copy-start.14 = (f32[2048]{0:T(1024)}, f32[2048]{0:T(1024)S(1)}, u32[]{:S(2)}) copy-start(f32[2048]{0:T(1024)S(1)} %get-tuple-element.37) | copy-start | bytes 24580
  116.8 29.2 %copy-start.12 = (f32[2048]{0:T(1024)}, f32[2048]{0:T(1024)S(1)}, u32[]{:S(2)}) copy-start(f32[2048]{0:T(1024)S(1)} %add_rsqrt_fusion) | copy-start | bytes 24580
  116.8 29.2 %copy-start.4 = (bf16[2048,768]{0,1:T(8,128)(2,1)S(1)}, bf16[2048,768]{0,1:T(8,128)(2,1)}, u32[]{:S(2)}) copy-start(bf16[2048,768]{0,1:T(8,128)(2,1)} %get-tuple-element.38) | copy-start | bytes 9437188
  146.0 29.2 %copy-start.3 = (bf16[1,2048,768]{2,1,0:T(8,128)(2,1)S(1)}, bf16[1,2048,768]{2,1,0:T(8,128)(2,1)}, u32[]{:S(2)}) copy-start(bf16[1,2048,768]{2,1,0:T(8,128)(2,1)} %param.12) | copy-start | bytes 9437188
  265.3 27.9 %copy-start.15 = (f32[2048]{0:T(1024)S(1)}, f32[2048]{0:T(1024)}, u32[]{:S(2)}) copy-start(f32[2048]{0:T(1024)} %copy-done.14) | copy-start | bytes 24580
  265.3 27.9 %copy-start.2 = (bf16[1,2048,768]{1,2,0:T(8,128)(2,1)S(1)}, bf16[1,2048,768]{1,2,0:T(8,128)(2,1)}, u32[]{:S(2)}) copy-start(bf16[1,2048,768]{1,2,0:T(8,128)(2,1)} %copy.21) | copy-start | bytes 9437188
  265.3 27.9 %copy-start.13 = (f32[2048]{0:T(1024)S(1)}, f32[2048]{0:T(1024)}, u32[]{:S(2)}) copy-start(f32[2048]{0:T(1024)} %copy-done.12) | copy-start | bytes 24580
  298.3 1.7 copy-start.6
  326.9 280.5 %reduce-scatter.17.cloned.1.call-start = ((), (), s32[]{:S(2)}) async-start(), calls=%async_computation.16 | async-start | bytes 9732096 | tf_op jit(solution)/shard_map/reduce_scatter | solution.py:63
  369.1 1.9 copy-start.5
  369.1 379.6 %reduce-scatter.13.cloned.1.call-start = ((), (), s32[]{:S(2)}) async-start(), calls=%async_computation.12 | async-start | bytes 9732096 | tf_op jit(solution)/shard_map/reduce_scatter | solution.py:63
  396.1 27.0 %copy-start.1 = (bf16[1,2048,768]{1,2,0:T(8,128)(2,1)S(1)}, bf16[1,2048,768]{1,2,0:T(8,128)(2,1)}, u32[]{:S(2)}) copy-start(bf16[1,2048,768]{1,2,0:T(8,128)(2,1)} %copy-done) | copy-start | bytes 9437188
  396.2 26.9 %copy-start.17 = (f32[2048]{0:T(1024)S(1)}, f32[2048]{0:T(1024)}, u32[]{:S(2)}) copy-start(f32[2048]{0:T(1024)} %copy-done.16) | copy-start | bytes 24580
  396.2 494.3 %reduce-scatter.11.cloned.1.call-start = ((), (), s32[]{:S(2)}) async-start(), calls=%async_computation.10 | async-start | bytes 9732096 | tf_op jit(solution)/shard_map/reduce_scatter | solution.py:63
  455.3 576.4 %reduce-scatter.9.cloned.1.call-start = ((), (), s32[]{:S(2)}) async-start(), calls=%async_computation.8 | async-start | bytes 9732096 | tf_op jit(solution)/shard_map/reduce_scatter | solution.py:63
  481.5 691.9 %reduce-scatter.7.cloned.1.call-start = ((), (), s32[]{:S(2)}) async-start(), calls=%async_computation.6 | async-start | bytes 9732096 | tf_op jit(solution)/shard_map/reduce_scatter | solution.py:63
  528.0 729.0 %all-gather.15.cloned.1.call-start = ((), (), s32[]{:S(2)}) async-start(), calls=%async_computation.15 | async-start | bytes 9732096 | tf_op jit(solution)/shard_map/all_gather | solution.py:68
  528.0 79.4 %copy-start.11 = (f32[2,192,768]{2,1,0:T(8,128)S(1)}, f32[2,192,768]{2,1,0:T(8,128)}, u32[]{:S(2)}) copy-start(f32[2,192,768]{2,1,0:T(8,128)} %param.18) | copy-start | bytes 3538948
  610.5 729.8 %all-gather.17.cloned.1.call-start = ((), (), s32[]{:S(2)}) async-start(), calls=%async_computation.17 | async-start | bytes 9732096 | tf_op jit(solution)/shard_map/all_gather | solution.py:68
  611.3 812.4 %all-gather.11.cloned.1.call-start = ((), (), s32[]{:S(2)}) async-start(), calls=%async_computation.11 | async-start | bytes 9732096 | tf_op jit(solution)/shard_map/all_gather | solution.py:68
  894.2 612.7 %all-gather.13.cloned.1.call-start = ((), (), s32[]{:S(2)}) async-start(), calls=%async_computation.13 | async-start | bytes 9732096 | tf_op jit(solution)/shard_map/all_gather | solution.py:68
  894.8 695.5 %all-gather.7.cloned.1.call-start = ((), (), s32[]{:S(2)}) async-start(), calls=%async_computation.7 | async-start | bytes 9732096 | tf_op jit(solution)/shard_map/all_gather | solution.py:68
  1177.2 496.3 %all-gather.9.cloned.1.call-start = ((), (), s32[]{:S(2)}) async-start(), calls=%async_computation.9 | async-start | bytes 9732096 | tf_op jit(solution)/shard_map/all_gather | solution.py:68
  1177.8 4.4 copy-start.7
  1177.8 4.4 copy-start.8
  1177.8 4.4 copy-start.9
  1177.9 4.4 copy-start.10
Sparse Core Ops, SparseCore 0:
  327.0 139.0 reduce-scatter.14
  472.0 135.4 reduce-scatter.16
  613.4 135.3 reduce-scatter.12
  755.0 135.3 reduce-scatter.10
  896.2 135.4 reduce-scatter.8
  1038.0 135.2 reduce-scatter.6
  1176.4 80.4 all-gather.14
  1260.0 80.2 all-gather.16
  1343.4 80.2 all-gather.10
  1426.6 80.2 all-gather.12
  1510.0 80.2 all-gather.6
  1593.2 80.2 all-gather.8

commit v2 on v0

v2 whole, which is shorter than its diff:
```python
import functools

import jax
import jax.numpy as jnp
from jax import lax
from jax.experimental import pallas as pl
from jax.experimental.pallas import tpu as pltpu
from jax.sharding import PartitionSpec as P

BF = jnp.bfloat16
F32 = jnp.float32
MESH = pl.DeviceIdType.MESH
NN, NT = ((1,), (0,)), ((1,), (1,))

CORE, Z0, Z1, Y, X = 1, 2, 4, 8, 16
ORDERS = ((CORE, X, Z0, Y, Z1), (CORE, Y, Z0, X, Z1))
STAGES = 5
CHUNKS = 6
PARTS = 3
PIECES = 2 * (CHUNKS + PARTS)
FRONT = 4


def dot(a, b, dims=NN):
    return lax.dot_general(a, b, (dims, ((), ())), preferred_element_type=F32)


def bit_of(i, bit):
    return (i // bit) % 2


def place(i, order):
    at = 0
    for bit in order:
        at = at * 2 + bit_of(i, bit)
    return at


def sigmoid(x):
    return 1.0 / (1.0 + jnp.exp(-x))


def normed(h):
    wide = h.astype(F32)
    return (wide * lax.rsqrt(jnp.mean(wide**2, -1, keepdims=True) + 1e-6)).astype(BF)


def adamw(w, m, v, g):
    m = 0.9 * m + 0.1 * g
    v = 0.95 * v + 0.05 * g * g
    step = m * lax.rsqrt(v + 1e-8) + 0.1 * w
    return (w - 0.02 * step).astype(BF), m, v


def forward_kernel(x_ref, wg_ref, wu_ref, wd_ref, p_ref, h_ref, a_all, total):
    chunk, tile = pl.program_id(0), pl.program_id(1)
    rows = p_ref.shape[0]
    here = pl.ds(pl.multiple_of(tile * rows, rows), rows)

    @pl.when(chunk == 0)
    def _():
        a_all[here, :] = normed(x_ref[here, :])

    a = a_all[here, :]
    gate, up = dot(a, wg_ref[...]), dot(a, wu_ref[...])
    p = (gate * sigmoid(gate) * up).astype(BF)
    p_ref[...] = p

    @pl.when(chunk == 0)
    def _():
        total[here, :] = dot(p, wd_ref[...])

    @pl.when(chunk > 0)
    def _():
        total[here, :] += dot(p, wd_ref[...])

    @pl.when(chunk == pl.num_programs(0) - 1)
    def _():
        down = total[here, :].astype(BF).astype(F32)
        h_ref[here, :] = (x_ref[here, :].astype(F32) + down).astype(BF)


def forward(x, wg, wu, wd, layer):
    tokens, d = x.shape
    ff = wg.shape[-1]
    c, rows = ff // CHUNKS, min(512, tokens)
    return pl.pallas_call(
        forward_kernel,
        name="forward",
        grid=(CHUNKS, tokens // rows),
        in_specs=[
            pl.BlockSpec((tokens, d), lambda i, t: (0, 0)),
            pl.BlockSpec((None, d, c), lambda i, t: (layer, 0, i)),
            pl.BlockSpec((None, d, c), lambda i, t: (layer, 0, i)),
            pl.BlockSpec((None, c, d), lambda i, t: (layer, i, 0)),
        ],
        out_specs=[pl.BlockSpec((rows, c), lambda i, t: (t, i)), pl.BlockSpec((tokens, d), lambda i, t: (0, 0))],
        out_shape=[jax.ShapeDtypeStruct((tokens, ff), BF), jax.ShapeDtypeStruct((tokens, d), BF)],
        scratch_shapes=[pltpu.VMEM((tokens, d), BF), pltpu.VMEM((tokens, d), F32)],
        compiler_params=pltpu.CompilerParams(vmem_limit_bytes=60 << 20),
        cost_estimate=pl.CostEstimate(flops=6 * tokens * d * ff, bytes_accessed=60 << 20, transcendentals=0),
    )(x, wg, wu, wd)


def step_kernel(
    x_hbm, dy_hbm, h_hbm, p0_hbm, wg_hbm, wu_hbm, wd_hbm, mg_hbm, mu_hbm, md_hbm, vg_hbm, vu_hbm, vd_hbm,
    wa_out, wb_out, mg_out, mu_out, md_out, vg_out, vu_out, vd_out, p1_hbm,
    a, at, dh, dht, wg, wu, wd, dg, du, ps, da, ga, gb, *rest,
):
    (ra, rb, sa, sb), rest = (rest[0:5], rest[5:10], rest[10:14], rest[14:18]), rest[18:]
    wn, mo, vo, wo, mo_d, vo_d, wo_d, rest = *rest[:7], rest[7:]
    rs_send, rs_recv, ag_send, ag_recv, own_sem, load_sem, w_sem, p_sem, opt_sem = rest

    tokens, d = a.shape
    c = wg.shape[1]
    r = d // 32
    e = d // PARTS
    rows = ps.shape[1]
    tiles = tokens // rows
    wide = 4 * 8 * r
    me = lax.axis_index("dp")
    g_bufs, r_bufs, s_bufs, w_outs = (ga, gb), (ra, rb), (sa, sb), (wa_out, wb_out)
    mine = [place(me, order) for order in ORDERS]

    barrier = pltpu.get_barrier_semaphore()
    for bit in (CORE, Z0, Z1, Y, X):
        other = me + bit * (1 - 2 * bit_of(me, bit))
        pl.semaphore_signal(barrier, inc=1, device_id={"dp": other}, device_id_type=MESH)
    pl.semaphore_wait(barrier, 5)

    def rs_copy(half, stage, parity):
        bit = ORDERS[half][stage]
        own, n = bit_of(me, bit), 16 >> stage
        source = g_bufs[half].at[parity] if stage == 0 else s_bufs[half][stage - 1]
        return pltpu.make_async_remote_copy(
            src_ref=source.at[pl.ds((1 - own) * n, n)],
            dst_ref=r_bufs[half][stage].at[parity],
            send_sem=rs_send.at[half, stage],
            recv_sem=rs_recv.at[half, stage, parity],
            device_id={"dp": me + bit * (1 - 2 * own)},
            device_id_type=MESH,
        )

    def rs_start(stage, piece):
        for half in range(2):
            rs_copy(half, stage, piece % 2).start()

    def rs_finish(stage, piece):
        for half in range(2):
            copy = rs_copy(half, stage, piece % 2)
            copy.wait_send()
            copy.wait_recv()
        for half in range(2):
            own, n = bit_of(me, ORDERS[half][stage]), 16 >> stage
            source = g_bufs[half].at[piece % 2] if stage == 0 else s_bufs[half][stage - 1]
            got, to = r_bufs[half][stage].at[piece % 2], s_bufs[half][stage]

            def add(i, _, source=source, got=got, to=to, own=own, n=n):
                to[i] = (source[own * n + i].astype(F32) + got[i].astype(F32)).astype(BF)
                return 0

            lax.fori_loop(0, n, add, 0)

    def rs_sum(half, piece):
        stage = STAGES - 1
        own = bit_of(me, ORDERS[half][stage])
        total = s_bufs[half][stage - 1][own].astype(F32) + r_bufs[half][stage][piece % 2, 0].astype(F32)
        return total.astype(BF).astype(F32)

    def ag_copy(half, stage, piece):
        bit = ORDERS[half][STAGES - 1 - stage]
        n = 1 << stage
        if stage == 0:
            source, to = wn.at[half], w_outs[half].at[piece, mine[half]]
        else:
            source = to = w_outs[half].at[piece, pl.ds((mine[half] // n) * n, n)]
        return pltpu.make_async_remote_copy(
            src_ref=source,
            dst_ref=to,
            send_sem=ag_send.at[half, stage],
            recv_sem=ag_recv.at[half, stage, piece % 2],
            device_id={"dp": me + bit * (1 - 2 * bit_of(me, bit))},
            device_id_type=MESH,
        )

    def own_copy(half, piece):
        return pltpu.make_async_copy(wn.at[half], w_outs[half].at[piece, mine[half]], own_sem.at[half])

    def ag_start(stage, piece):
        for half in range(2):
            ag_copy(half, stage, piece).start()
            if stage == 0:
                own_copy(half, piece).start()

    def ag_finish(stage, piece):
        for half in range(2):
            copy = ag_copy(half, stage, piece)
            copy.wait_send()
            copy.wait_recv()
            if stage == 0:
                own_copy(half, piece).wait()

    def is_wide(piece):
        return jnp.logical_or(piece < CHUNKS, piece >= CHUNKS + 2 * PARTS)

    def layer_of(piece):
        return jnp.where(piece < CHUNKS + PARTS, 1, 0)

    def chunk_of(piece):
        return jnp.where(piece < CHUNKS, piece, piece - CHUNKS - 2 * PARTS)

    def part_of(piece):
        return jnp.where(piece < CHUNKS + PARTS, piece - CHUNKS, piece - CHUNKS - PARTS)

    def opt_copies(piece, out):
        layer = layer_of(piece)
        cols = pl.ds(pl.multiple_of(chunk_of(piece) * c, c), c)
        part = pl.ds(pl.multiple_of(part_of(piece) * e, e), e)
        copies_wide, copies_part = [], []
        for half in range(2):
            here = pl.ds(half * 4 * r, 4 * r)
            for k, (hbm, hbm_out, vmem) in enumerate((((mg_hbm, mu_hbm)[half], (mg_out, mu_out)[half], mo), ((vg_hbm, vu_hbm)[half], (vg_out, vu_out)[half], vo))):
                if out:
                    copies_wide.append((vmem.at[half], hbm_out.at[layer, :, cols], opt_sem.at[half, k]))
                else:
                    copies_wide.append((hbm.at[layer, :, cols], vmem.at[half], opt_sem.at[half, k]))
            for k, (hbm, hbm_out, vmem) in enumerate(((md_hbm, md_out, mo_d), (vd_hbm, vd_out, vo_d))):
                if out:
                    copies_part.append((vmem.at[half], hbm_out.at[layer, here, part], opt_sem.at[half, k]))
                else:
                    copies_part.append((hbm.at[layer, here, part], vmem.at[half], opt_sem.at[half, k]))
            if not out:
                row = pl.multiple_of(me * r, 8)
                copies_wide.append(((wg_hbm, wu_hbm)[half].at[layer, pl.ds(row, r), cols], wo.at[half], opt_sem.at[half, 2]))
                row = pl.multiple_of(me * 8 * r + half * 4 * r, 8)
                copies_part.append((wd_hbm.at[layer, pl.ds(row, 4 * r), part], wo_d.at[half], opt_sem.at[half, 2]))
        return ((is_wide(piece), copies_wide), (jnp.logical_not(is_wide(piece)), copies_part))

    def opt_do(piece, out, start):
        for condition, copies in opt_copies(piece, out):

            @pl.when(condition)
            def _(copies=copies):
                for source, to, sem in copies:
                    copy = pltpu.make_async_copy(source, to, sem)
                    copy.start() if start else copy.wait()

    def opt_step(piece):
        @pl.when(is_wide(piece))
        def _():
            for half in range(2):
                w, m, v = adamw(wo[half].astype(F32), mo[half], vo[half], rs_sum(half, piece))
                wn[half], mo[half], vo[half] = w, m, v

        @pl.when(jnp.logical_not(is_wide(piece)))
        def _():
            for half in range(2):
                g = rs_sum(half, piece)
                for j in range(4):
                    at_rows, at_cols = pl.ds(j * r, r), pl.ds(j * e, e)
                    w, m, v = adamw(
                        wo_d[half, at_rows, :].astype(F32), mo_d[half, at_rows, :], vo_d[half, at_rows, :], g[:, j * e : (j + 1) * e]
                    )
                    wn[half, :, at_cols], mo_d[half, at_rows, :], vo_d[half, at_rows, :] = w, m, v

    def active(piece):
        return jnp.logical_and(piece >= 0, piece < PIECES)

    def service(k, point):
        one, two, three, four = k - 1, k - 2, k - 3, k - 4
        if point == 0:

            @pl.when(active(one))
            def _():
                rs_start(0, one)

            @pl.when(active(three))
            def _():
                ag_finish(0, three)
                ag_start(1, three)
                opt_do(three, True, False)

            @pl.when(active(two))
            def _():
                opt_do(two, False, True)

        if point == 1:

            @pl.when(active(one))
            def _():
                rs_finish(0, one)
                rs_start(1, one)

            @pl.when(active(two))
            def _():
                rs_finish(2, two)
                rs_start(3, two)

            @pl.when(active(three))
            def _():
                ag_finish(1, three)
                ag_start(2, three)

            @pl.when(active(four))
            def _():
                ag_finish(3, four)
                ag_start(4, four)

        if point == 2:

            @pl.when(active(two))
            def _():
                rs_finish(3, two)
                rs_start(4, two)

            @pl.when(active(four))
            def _():
                ag_finish(4, four)

        if point == 3:

            @pl.when(active(one))
            def _():
                rs_finish(1, one)
                rs_start(2, one)

            @pl.when(active(two))
            def _():
                for half in range(2):
                    copy = rs_copy(half, STAGES - 1, two % 2)
                    copy.wait_send()
                    copy.wait_recv()
                opt_do(two, False, False)
                opt_step(two)
                opt_do(two, True, True)
                ag_start(0, two)

            @pl.when(active(three))
            def _():
                ag_finish(2, three)
                ag_start(3, three)

    def w_copy(which, piece):
        layer, at_cols = layer_of(piece), pl.ds(pl.multiple_of(chunk_of(piece) * c, c), c)
        if which == 2:
            return pltpu.make_async_copy(wd_hbm.at[layer, at_cols, :], wd, w_sem.at[2])
        return pltpu.make_async_copy((wg_hbm, wu_hbm)[which].at[layer, :, at_cols], (wg, wu)[which], w_sem.at[which])

    def p_copy(piece, tile):
        slot = tile % 2
        at_cols = pl.ds(pl.multiple_of(chunk_of(piece) * c, c), c)
        return pltpu.make_async_copy(ps.at[slot], p1_hbm.at[pl.ds(pl.multiple_of(tile * rows, rows), rows), at_cols], p_sem.at[slot])

    def front_tile(piece, tile):
        here = pl.ds(pl.multiple_of(tile * rows, rows), rows)
        at_, dh_ = a[here, :], dh[here, :]
        @pl.when(jnp.logical_and(layer_of(piece) == 1, tile >= 2))
        def _():
            p_copy(piece, tile - 2).wait()

        n = c // FRONT
        for j in range(FRONT):
            cols = slice(j * n, (j + 1) * n)
            gate, up = dot(at_, wg[:, cols]), dot(at_, wu[:, cols])
            dp = dot(dh_, wd[cols, :], NT).astype(BF).astype(F32)
            s = sigmoid(gate)
            gs = gate * s
            ps[tile % 2, :, cols] = (gs * up).astype(BF)
            du[here, cols] = (dp * gs).astype(BF)
            dg[here, cols] = (dp * up * (s * (1.0 + gate * (1.0 - s)))).astype(BF)

        @pl.when(layer_of(piece) == 1)
        def _():
            p_copy(piece, tile).start()

    def weight_part(which, piece):
        grads, to = (dg, du)[which], (ga, gb)[which]

        @pl.when(layer_of(piece) == 1)
        def _():
            def back(tile, _):
                here = pl.ds(pl.multiple_of(tile * rows, rows), rows)
                part = dot(grads[here, :], (wg, wu)[which][...], NT)
                if which == 0:
                    old = jnp.where(chunk_of(piece) == 0, jnp.zeros_like(part), da[here, :])
                    da[here, :] = old + part
                else:
                    da[here, :] += part
                return 0

            lax.fori_loop(0, tiles, back, 0)

        following = jnp.where(piece < CHUNKS - 1, piece + 1, jnp.where(piece < CHUNKS, CHUNKS + 2 * PARTS, piece + 1))

        @pl.when(following < PIECES)
        def _():
            w_copy(which, following).start()
            if which == 1:
                w_copy(2, following).start()

        n = c // 2
        for j in range(2):
            term = dot(at[...], grads[:, j * n : (j + 1) * n])
            for i in range(32):
                to[piece % 2, place(i, ORDERS[which]), :, j * n : (j + 1) * n] = term[i * r : (i + 1) * r, :].astype(BF)

    def tile_copy(piece, tile, source):
        return pltpu.make_async_copy(source.at[:, pl.ds(tile * wide, wide)], (dg, du)[tile % 2].at[:, pl.ds(0, wide)], load_sem.at[tile % 2])

    def tile_start(piece, tile):
        @pl.when(layer_of(piece) == 1)
        def _():
            tile_copy(piece, tile, p1_hbm).start()

        @pl.when(layer_of(piece) == 0)
        def _():
            tile_copy(piece, tile, p0_hbm).start()

    def down_tile(piece, tile):
        tile_copy(piece, tile, p0_hbm).wait()
        at_rows = pl.ds(pl.multiple_of(part_of(piece) * e, e), e)
        term = dot(dht[at_rows, :], (dg, du)[tile % 2][:, :wide]).T
        for i in range(4):
            for j in range(8):
                half, jj = j // 4, j % 4
                block = term[(8 * i + j) * r : (8 * i + j + 1) * r, :].astype(BF)
                g_bufs[half][piece % 2, place(4 * tile + i, ORDERS[half]), :, jj * e : (jj + 1) * e] = block
        if tile + 2 < 8:
            tile_start(piece, tile + 2)

    def through_norm():
        def back(tile, _):
            here = pl.ds(pl.multiple_of(tile * rows, rows), rows)
            load = pltpu.make_async_copy(h_hbm.at[here, :], ps.at[0, :, pl.ds(0, d)], p_sem.at[0])
            load.start()
            load.wait()

            def some(i, _):
                at_rows = pl.ds(pl.multiple_of(i * 32, 32), 32)
                at_all = pl.ds(pl.multiple_of(tile * rows + i * 32, 32), 32)
                h = ps[0, at_rows, pl.ds(0, d)].astype(F32)
                by_a = da[at_all, :].astype(BF).astype(F32)
                scale = lax.rsqrt(jnp.mean(h * h, -1, keepdims=True) + 1e-6)
                along = jnp.sum(by_a * h, -1, keepdims=True)
                by_h = (by_a * scale - h * (scale * scale * scale * along * (1.0 / d))).astype(BF)
                dh[at_all, :] = (dh[at_all, :].astype(F32) + by_h.astype(F32)).astype(BF)
                return 0

            lax.fori_loop(0, rows // 32, some, 0)
            return 0

        lax.fori_loop(0, tiles, back, 0)

    def turn(source, to):
        def back(tile, _):
            here = pl.ds(pl.multiple_of(tile * rows, rows), rows)
            to[:, here] = source[here, :].astype(F32).T.astype(BF)
            return 0

        lax.fori_loop(0, tiles, back, 0)

    def norm_all():
        def back(i, _):
            here = pl.ds(pl.multiple_of(i * 32, 32), 32)
            a[here, :] = normed(a[here, :])
            return 0

        lax.fori_loop(0, tokens // 32, back, 0)
        turn(a, at)

    first = (
        pltpu.make_async_copy(h_hbm, a, load_sem.at[2]),
        pltpu.make_async_copy(dy_hbm, dh, load_sem.at[3]),
        *(w_copy(which, 0) for which in range(3)),
    )
    for copy in first:
        copy.start()
    first[0].wait()
    norm_all()
    first[1].wait()
    turn(dh, dht)
    x_copy = pltpu.make_async_copy(x_hbm, a, load_sem.at[2])

    def tick(k, _):
        computes = k < PIECES
        gated = jnp.logical_and(computes, is_wide(k))
        downs = jnp.logical_and(computes, jnp.logical_not(is_wide(k)))

        @pl.when(downs)
        def _():
            tile_start(k, 0)
            tile_start(k, 1)

        for point in range(4):
            service(k, point)

            @pl.when(gated)
            def _(point=point):
                if point == 0:
                    for which in range(3):
                        w_copy(which, k).wait()
                if point < 2:

                    def front(i, _):
                        front_tile(k, i + point * (tiles // 2))
                        return 0

                    lax.fori_loop(0, tiles // 2, front, 0)
                else:
                    weight_part(point - 2, k)
                if point == 3:

                    @pl.when(layer_of(k) == 1)
                    def _():
                        p_copy(k, tiles - 2).wait()
                        p_copy(k, tiles - 1).wait()

            @pl.when(downs)
            def _(point=point):
                down_tile(k, 2 * point)
                down_tile(k, 2 * point + 1)

        @pl.when(k == CHUNKS - 1)
        def _():
            x_copy.start()

        @pl.when(k == CHUNKS + PARTS - 1)
        def _():
            through_norm()
            turn(dh, dht)
            x_copy.wait()
            norm_all()

        return 0

    lax.fori_loop(0, PIECES + 4, tick, 0)


def train_step(x, dy, h, p0, weights, ms, vs):
    tokens, d = dy.shape
    ff = p0.shape[1]
    c, r, e = ff // CHUNKS, d // 32, d // PARTS
    rows = min(512, tokens // 4)
    any_ = pl.BlockSpec(memory_space=pl.ANY)
    blocks = lambda *n: pltpu.VMEM((*n, r, c), BF)
    scratch = [
        pltpu.VMEM((tokens, d), BF), pltpu.VMEM((d, tokens), BF), pltpu.VMEM((tokens, d), BF), pltpu.VMEM((d, tokens), BF),
        pltpu.VMEM((d, c), BF), pltpu.VMEM((d, c), BF), pltpu.VMEM((c, d), BF),
        pltpu.VMEM((tokens, c), BF), pltpu.VMEM((tokens, c), BF),
        pltpu.VMEM((2, rows, c), BF),
        pltpu.VMEM((tokens, d), F32),
        blocks(2, 32), blocks(2, 32),
        *[blocks(2, 16 >> s) for s in range(STAGES)] * 2,
        *[blocks(16 >> s) for s in range(STAGES - 1)] * 2,
        blocks(2), pltpu.VMEM((2, r, c), F32), pltpu.VMEM((2, r, c), F32), blocks(2),
        pltpu.VMEM((2, 4 * r, e), F32), pltpu.VMEM((2, 4 * r, e), F32), pltpu.VMEM((2, 4 * r, e), BF),
        pltpu.SemaphoreType.DMA((2, STAGES)), pltpu.SemaphoreType.DMA((2, STAGES, 2)),
        pltpu.SemaphoreType.DMA((2, STAGES)), pltpu.SemaphoreType.DMA((2, STAGES, 2)),
        pltpu.SemaphoreType.DMA((2,)), pltpu.SemaphoreType.DMA((4,)), pltpu.SemaphoreType.DMA((3,)), pltpu.SemaphoreType.DMA((2,)),
        pltpu.SemaphoreType.DMA((2, 3)),
    ]
    packed = jax.ShapeDtypeStruct((PIECES, 32, r, c), BF)
    like = [jax.ShapeDtypeStruct(t.shape, F32) for t in (*ms, *vs)]
    return pl.pallas_call(
        step_kernel,
        name="step",
        in_specs=[any_] * 13,
        out_specs=[any_] * 9,
        out_shape=[packed, packed, *like, jax.ShapeDtypeStruct((tokens, ff), BF)],
        scratch_shapes=scratch,
        compiler_params=pltpu.CompilerParams(collective_id=0, has_side_effects=True, vmem_limit_bytes=67_000_000),
        cost_estimate=pl.CostEstimate(flops=28 * tokens * d * ff, bytes_accessed=400 << 20, transcendentals=0),
    )(x, dy, h, p0, *weights, *ms, *vs)


def unpack_kernel(gate_ref, up_ref, down_a, down_b, wg_ref, wu_ref, wd_ref):
    r, c = gate_ref.shape[-2:]
    e = c // 4
    for core in range(2):
        for z0 in range(2):
            for z1 in range(2):
                owner = z1 * 4 + z0 * 2 + core
                for chunk in range(CHUNKS):
                    at_cols = pl.ds(chunk * c, c)
                    wg_ref[pl.ds(owner * r, r), at_cols] = gate_ref[chunk, core, z0, z1]
                    wu_ref[pl.ds(owner * r, r), at_cols] = up_ref[chunk, core, z0, z1]
                for part in range(PARTS):
                    for half, ref in enumerate((down_a, down_b)):
                        for j in range(4):
                            at_rows = pl.ds(owner * 8 * r + (half * 4 + j) * r, r)
                            wd_ref[at_rows, pl.ds(part * e, e)] = ref[part, core, z0, z1, :, pl.ds(j * e, e)]


def unpack(wa, wb, d, ff):
    r, c = wa.shape[-2:]
    wa, wb = (t.reshape(PIECES, *(2,) * 5, r, c) for t in (wa, wb))
    block = (None, 2, None, 2, r, c)

    def spec(n, first, half):
        def index(layer, x, y):
            outer, inner = (x, y) if half == 0 else (y, x)
            return (first(layer), 0, outer, 0, inner, 0, 0, 0)

        return pl.BlockSpec((n, 2, None, 2, None, 2, r, c), index)

    wide, part = lambda layer: 2 - 2 * layer, lambda layer: 3 - layer
    return pl.pallas_call(
        unpack_kernel,
        name="unpack",
        grid=(2, 2, 2),
        in_specs=[spec(CHUNKS, wide, 0), spec(CHUNKS, wide, 1), spec(PARTS, part, 0), spec(PARTS, part, 1)],
        out_specs=[
            pl.BlockSpec((None, d // 4, ff), lambda layer, x, y: (layer, 2 * x + y, 0)),
            pl.BlockSpec((None, d // 4, ff), lambda layer, x, y: (layer, 2 * x + y, 0)),
            pl.BlockSpec((None, ff // 4, d), lambda layer, x, y: (layer, 2 * x + y, 0)),
        ],
        out_shape=[jax.ShapeDtypeStruct((2, d, ff), BF)] * 2 + [jax.ShapeDtypeStruct((2, ff, d), BF)],
        compiler_params=pltpu.CompilerParams(vmem_limit_bytes=60 << 20),
    )(wa, wb, wa, wb)


def solution(mesh):
    def step(x, dy, *arrays):
        wg, wu, wd = arrays[:3]
        ms, vs = arrays[3:6], arrays[6:9]
        x, dy = x[0], dy[0]
        p0, h = forward(x, wg, wu, wd, 0)
        wa, wb, *moments, _ = train_step(x, dy, h, p0, (wg, wu, wd), ms, vs)
        return (*unpack(wa, wb, x.shape[1], wg.shape[2]), *moments)

    seq, whole, rows = P(("rep", "dp")), P(), P(None, "dp")
    return jax.shard_map(
        step,
        mesh=mesh,
        in_specs=(seq, seq) + (whole,) * 3 + (rows,) * 6,
        out_specs=(P("rep"),) * 3 + (P("rep", "dp"),) * 6,
        check_vma=False,
    )
```

time: 2920 us -> 761 us (0.26)
  matrix products: 1210 us -> 0 us
  Pallas kernels: 0 us -> 750 us
  waiting for transfers between devices: 538 us -> 0 us
  starting transfers between devices: 536 us -> 0 us
  other arithmetic: 491 us -> 0 us
  local copies, waits for them, and re-layouts: 114 us -> 9.49 us
    dot_general x105 -> x0, matrix products: 1210 us -> none  [the longest x35 512 us: layer(): gate = jnp.dot(a, w['w_gate'], preferred_element_type=jnp.float32)]
    pallas_call x0 -> x3, Pallas kernels: none -> 750 us  [the longest x1 637 us: train_step(): pl.pallas_call(step_kernel, name='step', in_specs=[any_] * 13, out_specs=...]
    dot_general x198 -> x0, starting transfers between devices: 536 us -> none  [the longest x66 191 us: layer(): gate = jnp.dot(a, w['w_gate'], preferred_element_type=jnp.float32)]
    dot_general x192 -> x0, other arithmetic: 424 us -> none
    dot_general x198 -> x0, waiting for transfers between devices: 418 us -> none  [the longest x66 305 us: matmul(): jnp.dot(a, w, preferred_element_type=jnp.float32).astype(jnp.bfloat16)]
    reshape x3 -> x0, waiting for transfers between devices: 120 us -> none  [step(): t.reshape(-1, *t.shape[2:])]
    unnamed x56 -> x18, local copies, waits for them, and re-layouts: 114 us -> 9.49 us
    convert_element_type x3 -> x0, other arithmetic: 43.6 us -> none  [the longest x1 40.1 us: layer(): (jax.nn.silu(gate) * up).astype(jnp.bfloat16)]
  transfers between devices with their start and end apart: 201 -> 0, of which waited for: 67 -> 0; matrix products, arithmetic and copies ran while one was open for 48% -> 0% of each run, Pallas kernels for 0% -> 0%
where the time goes in v2:
time: 761 us; the launch traced here: 760 us
  Pallas kernels  750 us (99%)
  local copies, waits for them, and re-layouts  9.49 us (1%)
    pallas_call x1, Pallas kernels, train_step(): pl.pallas_call(step_kernel, name='step', in_specs=[any_] * 13, out_specs=...  637 us
    pallas_call x1, Pallas kernels, forward(): pl.pallas_call(forward_kernel, name='forward', grid=(CHUNKS, tokens // ro...  76.3 us
    pallas_call x1, Pallas kernels, unpack(): pl.pallas_call(unpack_kernel, name='unpack', grid=(2, 2, 2), in_specs=[sp...  36.3 us

profile of v2, /device:TPU:0, one launch (start us, length us, event | category | flops | bytes accessed | tf_op | source)
XLA Modules:
  0.0 760.1 jit_solution(1557837488192846420)
XLA Ops:
  0.6 76.3 %forward.1 = (bf16[2048,6144]{1,0:T(8,128)(2,1)}, bf16[2048,768]{1,0:T(8,128)(2,1)}) custom-call(bf16[2048,768]{1,0:T(8,128)(2,1)} %bitcast.8, bf16[2,768,6144]{2,1,0:T(8,128)(2,1)} %wg_hbm.1, bf16[2,768,6144]{2,1,0:T(8,128)(2,1)} %wu_hbm.1, bf16[2,6144,768]{2,1,0:T(8,128)(2,1)} %wd_hbm.1), custom_call_target="tpu_custom_call" | custom-call | flops 57982058496 | bytes 62914560 | tf_op jit(solution)/shard_map/forward/pallas_call | solution.py:87
  76.9 637.4 %step.1 = (bf16[18,32,24,1024]{3,2,1,0:T(8,128)(2,1)}, bf16[18,32,24,1024]{3,2,1,0:T(8,128)(2,1)}, f32[2,24,6144]{2,1,0:T(8,128)}, f32[2,24,6144]{2,1,0:T(8,128)...) custom-call(bf16[2048,768]{1,0:T(8,128)(2,1)} %bitcast.9, ...), custom_call_target="tpu_custom_call" | custom-call | flops 270582939648 | bytes 419430400 | tf_op jit(solution)/shard_map/step/pallas_call | solution.py:564
  714.4 0.0 copy-start.5
  714.4 36.3 %unpack.1 = (bf16[2,768,6144]{2,1,0:T(8,128)(2,1)}, bf16[2,768,6144]{2,1,0:T(8,128)(2,1)}, bf16[2,6144,768]{2,1,0:T(8,128)(2,1)}) custom-call(bf16[18,2,2,2,2,2,24,1024]{7,6,5,4,3,2,1,0:T(8,128)(2,1)} %bitcast.4, bf16[18,2,2,2,2,2,24,1024]{7,6,5,4,3,2,1,0:T(8,128)(2,1)} %bitcast.6, bf16[18,2,2,2,2,2,24,1024]{7,6,5,4,3,2,1,0:T(8,128)(2,1)} %bitcast.5, ...), custom_call_target="tpu_custom_call" | custom-call | tf_op jit(solution)/shard_map/unpack/pallas_call | solution.py:607
  750.6 0.0 copy-done.5
  750.6 0.0 copy-start.4
  750.6 1.0 copy.26
  751.7 0.7 copy-done.4
  752.3 0.0 copy-start.3
  752.3 1.0 copy.27
  753.3 0.7 copy-done.3
  754.0 0.0 copy-start.2
  754.0 1.0 copy.28
  755.0 0.7 copy-done.2
  755.7 0.0 copy-start.1
  755.7 1.0 copy.29
  756.7 0.7 copy-done.1
  757.4 0.0 copy-start
  757.4 1.0 copy.30
  758.4 0.7 copy-done
  759.1 1.0 copy.31
Async XLA Ops:
  714.4 36.3 %copy-start.5 = (f32[2,24,6144]{2,1,0:T(8,128)S(1)}, f32[2,24,6144]{2,1,0:T(8,128)}, u32[]{:S(2)}) copy-start(f32[2,24,6144]{2,1,0:T(8,128)} %get-tuple-element.47) | copy-start | bytes 3538948
  750.6 1.7 copy-start.4
  752.3 1.7 copy-start.3
  754.0 1.7 copy-start.2
  755.7 1.7 copy-start.1
  757.4 1.7 copy-start

commit v3 on v2

--- a/solution.py
+++ b/solution.py
@@ -19,6 +19,14 @@
 PARTS = 3
 PIECES = 2 * (CHUNKS + PARTS)
 FRONT = 4
+SUBS = 4
+TIMES = (
+    (4, 5, 7, 9, 11, 12, 13, 14, 16, 19, 23),
+    (5, 6, 8, 10, 11, 12, 13, 17, 20, 23, 27),
+    (4, 7, 9, 11, 12, 13, 14, 15, 17, 20, 24),
+    (6, 8, 10, 12, 13, 14, 15, 16, 19, 22, 24),
+)
+TICKS = PIECES + max(t[-1] for t in TIMES) // 4
 
 
 def dot(a, b, dims=NN):
@@ -108,7 +116,7 @@
     a, at, dh, dht, wg, wu, wd, dg, du, ps, da, ga, gb, *rest,
 ):
     (ra, rb, sa, sb), rest = (rest[0:5], rest[5:10], rest[10:14], rest[14:18]), rest[18:]
-    wn, mo, vo, wo, mo_d, vo_d, wo_d, rest = *rest[:7], rest[7:]
+    wn, mo, vo, wo, *rest = rest
     rs_send, rs_recv, ag_send, ag_recv, own_sem, load_sem, w_sem, p_sem, opt_sem = rest
 
     tokens, d = a.shape
@@ -128,77 +136,82 @@
         pl.semaphore_signal(barrier, inc=1, device_id={"dp": other}, device_id_type=MESH)
     pl.semaphore_wait(barrier, 5)
 
-    def rs_copy(half, stage, parity):
+    def rs_copy(half, stage, piece, sub):
         bit = ORDERS[half][stage]
         own, n = bit_of(me, bit), 16 >> stage
-        source = g_bufs[half].at[parity] if stage == 0 else s_bufs[half][stage - 1]
+        source = g_bufs[half].at[piece % 2, sub] if stage == 0 else s_bufs[half][stage - 1].at[sub]
         return pltpu.make_async_remote_copy(
             src_ref=source.at[pl.ds((1 - own) * n, n)],
-            dst_ref=r_bufs[half][stage].at[parity],
-            send_sem=rs_send.at[half, stage],
-            recv_sem=rs_recv.at[half, stage, parity],
+            dst_ref=r_bufs[half][stage].at[piece % 2, sub],
+            send_sem=rs_send.at[half, stage, sub],
+            recv_sem=rs_recv.at[half, stage, sub, piece % 2],
             device_id={"dp": me + bit * (1 - 2 * own)},
             device_id_type=MESH,
         )
 
-    def rs_start(stage, piece):
+    def rs_start(stage, piece, sub):
         for half in range(2):
-            rs_copy(half, stage, piece % 2).start()
-
-    def rs_finish(stage, piece):
+            rs_copy(half, stage, piece, sub).start()
+
+    def rs_wait(stage, piece, sub):
         for half in range(2):
-            copy = rs_copy(half, stage, piece % 2)
+            copy = rs_copy(half, stage, piece, sub)
             copy.wait_send()
             copy.wait_recv()
+
+    def rs_add(stage, piece, sub):
+        n = 16 >> stage
+        some = min(n, 4)
         for half in range(2):
-            own, n = bit_of(me, ORDERS[half][stage]), 16 >> stage
-            source = g_bufs[half].at[piece % 2] if stage == 0 else s_bufs[half][stage - 1]
-            got, to = r_bufs[half][stage].at[piece % 2], s_bufs[half][stage]
-
-            def add(i, _, source=source, got=got, to=to, own=own, n=n):
-                to[i] = (source[own * n + i].astype(F32) + got[i].astype(F32)).astype(BF)
+            own = bit_of(me, ORDERS[half][stage])
+            source = g_bufs[half].at[piece % 2, sub] if stage == 0 else s_bufs[half][stage - 1].at[sub]
+            got, to = r_bufs[half][stage].at[piece % 2, sub], s_bufs[half][stage].at[sub]
+
+            def add(i, _, source=source, got=got, to=to, own=own):
+                here = pl.ds(i * some, some)
+                to[here] = (source[pl.ds(own * n + i * some, some)].astype(F32) + got[here].astype(F32)).astype(BF)
                 return 0
 
-            lax.fori_loop(0, n, add, 0)
-
-    def rs_sum(half, piece):
+            lax.fori_loop(0, n // some, add, 0)
+
+    def rs_sum(half, piece, sub):
         stage = STAGES - 1
         own = bit_of(me, ORDERS[half][stage])
-        total = s_bufs[half][stage - 1][own].astype(F32) + r_bufs[half][stage][piece % 2, 0].astype(F32)
+        total = s_bufs[half][stage - 1][sub, own].astype(F32) + r_bufs[half][stage][piece % 2, sub, 0].astype(F32)
         return total.astype(BF).astype(F32)
 
-    def ag_copy(half, stage, piece):
+    def ag_copy(half, stage, piece, sub):
         bit = ORDERS[half][STAGES - 1 - stage]
         n = 1 << stage
         if stage == 0:
-            source, to = wn.at[half], w_outs[half].at[piece, mine[half]]
+            source, to = wn.at[half, sub], w_outs[half].at[piece, sub, mine[half]]
         else:
-            source = to = w_outs[half].at[piece, pl.ds((mine[half] // n) * n, n)]
+            source = to = w_outs[half].at[piece, sub, pl.ds((mine[half] // n) * n, n)]
         return pltpu.make_async_remote_copy(
             src_ref=source,
             dst_ref=to,
-            send_sem=ag_send.at[half, stage],
-            recv_sem=ag_recv.at[half, stage, piece % 2],
+            send_sem=ag_send.at[half, stage, sub],
+            recv_sem=ag_recv.at[half, stage, sub, piece % 2],
             device_id={"dp": me + bit * (1 - 2 * bit_of(me, bit))},
             device_id_type=MESH,
         )
 
-    def own_copy(half, piece):
-        return pltpu.make_async_copy(wn.at[half], w_outs[half].at[piece, mine[half]], own_sem.at[half])
-
-    def ag_start(stage, piece):
+    def own_copy(half, piece, sub):
+        return pltpu.make_async_copy(wn.at[half, sub], w_outs[half].at[piece, sub, mine[half]], own_sem.at[half, sub])
+
+    def ag_start(stage, piece, sub):
         for half in range(2):
-            ag_copy(half, stage, piece).start()
+            ag_copy(half, stage, piece, sub).start()
             if stage == 0:
-                own_copy(half, piece).start()
-
-    def ag_finish(stage, piece):
+                own_copy(half, piece, sub).start()
+
+    def ag_finish(stage, piece, sub):
         for half in range(2):
-            copy = ag_copy(half, stage, piece)
+            copy = ag_copy(half, stage, piece, sub)
             copy.wait_send()
             copy.wait_recv()
             if stage == 0:
-                own_copy(half, piece).wait()
+                own_copy(half, piece, sub).wait()
 
     def is_wide(piece):
         return jnp.logical_or(piece < CHUNKS, piece >= CHUNKS + 2 * PARTS)
@@ -212,133 +225,78 @@
     def part_of(piece):
         return jnp.where(piece < CHUNKS + PARTS, piece - CHUNKS, piece - CHUNKS - PARTS)
 
-    def opt_copies(piece, out):
+    def opt_do(piece, sub, out, start):
         layer = layer_of(piece)
-        cols = pl.ds(pl.multiple_of(chunk_of(piece) * c, c), c)
-        part = pl.ds(pl.multiple_of(part_of(piece) * e, e), e)
-        copies_wide, copies_part = [], []
+        wide_cols = pl.ds(pl.multiple_of(chunk_of(piece) * c + sub * e, e), e)
+        part_cols = pl.ds(pl.multiple_of(part_of(piece) * e, e), e)
+
+        def copies(wide):
+            for half in range(2):
+                group = (half * SUBS + sub) * r
+                rows_, cols = (slice(None), wide_cols) if wide else (pl.ds(group, r), part_cols)
+                kinds = ((mg_hbm, mu_hbm)[half], mg_out if half == 0 else mu_out, mo), ((vg_hbm, vu_hbm)[half], vg_out if half == 0 else vu_out, vo)
+                if not wide:
+                    kinds = (md_hbm, md_out, mo), (vd_hbm, vd_out, vo)
+                for k, (hbm, hbm_out, vmem) in enumerate(kinds):
+                    sem = opt_sem.at[half, k, sub]
+                    if out:
+                        yield pltpu.make_async_copy(vmem.at[half, sub], hbm_out.at[layer, rows_, cols], sem)
+                    else:
+                        yield pltpu.make_async_copy(hbm.at[layer, rows_, cols], vmem.at[half, sub], sem)
+                if not out:
+                    own = me * r if wide else me * 8 * r + group
+                    source = (wg_hbm, wu_hbm)[half] if wide else wd_hbm
+                    own = pl.ds(pl.multiple_of(own, 8), r)
+                    yield pltpu.make_async_copy(source.at[layer, own, cols], wo.at[half, sub], opt_sem.at[half, 2, sub])
+
+        if not start:
+            for half in range(2):
+                for k, vmem in enumerate((mo, vo, wo)[: 2 if out else 3]):
+                    block = (mg_hbm, vg_hbm, wg_hbm)[k].at[0, pl.ds(0, r), pl.ds(0, e)]
+                    pltpu.make_async_copy(block, vmem.at[half, sub], opt_sem.at[half, k, sub]).wait()
+            return
+        for wide in (True, False):
+
+            @pl.when(is_wide(piece) == wide)
+            def _(wide=wide):
+                for copy in copies(wide):
+                    copy.start()
+
+    def opt_step(piece, sub):
         for half in range(2):
-            here = pl.ds(half * 4 * r, 4 * r)
-            for k, (hbm, hbm_out, vmem) in enumerate((((mg_hbm, mu_hbm)[half], (mg_out, mu_out)[half], mo), ((vg_hbm, vu_hbm)[half], (vg_out, vu_out)[half], vo))):
-                if out:
-                    copies_wide.append((vmem.at[half], hbm_out.at[layer, :, cols], opt_sem.at[half, k]))
-                else:
-                    copies_wide.append((hbm.at[layer, :, cols], vmem.at[half], opt_sem.at[half, k]))
-            for k, (hbm, hbm_out, vmem) in enumerate(((md_hbm, md_out, mo_d), (vd_hbm, vd_out, vo_d))):
-                if out:
-                    copies_part.append((vmem.at[half], hbm_out.at[layer, here, part], opt_sem.at[half, k]))
-                else:
-                    copies_part.append((hbm.at[layer, here, part], vmem.at[half], opt_sem.at[half, k]))
-            if not out:
-                row = pl.multiple_of(me * r, 8)
-                copies_wide.append(((wg_hbm, wu_hbm)[half].at[layer, pl.ds(row, r), cols], wo.at[half], opt_sem.at[half, 2]))
-                row = pl.multiple_of(me * 8 * r + half * 4 * r, 8)
-                copies_part.append((wd_hbm.at[layer, pl.ds(row, 4 * r), part], wo_d.at[half], opt_sem.at[half, 2]))
-        return ((is_wide(piece), copies_wide), (jnp.logical_not(is_wide(piece)), copies_part))
-
-    def opt_do(piece, out, start):
-        for condition, copies in opt_copies(piece, out):
-
-            @pl.when(condition)
-            def _(copies=copies):
-                for source, to, sem in copies:
-                    copy = pltpu.make_async_copy(source, to, sem)
-                    copy.start() if start else copy.wait()
-
-    def opt_step(piece):
-        @pl.when(is_wide(piece))
-        def _():
-            for half in range(2):
-                w, m, v = adamw(wo[half].astype(F32), mo[half], vo[half], rs_sum(half, piece))
-                wn[half], mo[half], vo[half] = w, m, v
-
-        @pl.when(jnp.logical_not(is_wide(piece)))
-        def _():
-            for half in range(2):
-                g = rs_sum(half, piece)
-                for j in range(4):
-                    at_rows, at_cols = pl.ds(j * r, r), pl.ds(j * e, e)
-                    w, m, v = adamw(
-                        wo_d[half, at_rows, :].astype(F32), mo_d[half, at_rows, :], vo_d[half, at_rows, :], g[:, j * e : (j + 1) * e]
-                    )
-                    wn[half, :, at_cols], mo_d[half, at_rows, :], vo_d[half, at_rows, :] = w, m, v
-
-    def active(piece):
-        return jnp.logical_and(piece >= 0, piece < PIECES)
+            w, m, v = adamw(wo[half, sub].astype(F32), mo[half, sub], vo[half, sub], rs_sum(half, piece, sub))
+            wn[half, sub], mo[half, sub], vo[half, sub] = w, m, v
+
+    def go_on(event, piece, sub):
+        if event < STAGES:
+            if event >= 0:
+                rs_wait(event, piece, sub)
+            if 0 <= event < STAGES - 1:
+                rs_add(event, piece, sub)
+            if event < STAGES - 1:
+                rs_start(event + 1, piece, sub)
+            if event == STAGES - 2:
+                opt_do(piece, sub, False, True)
+            if event == STAGES - 1:
+                opt_do(piece, sub, False, False)
+                opt_step(piece, sub)
+                opt_do(piece, sub, True, True)
+                ag_start(0, piece, sub)
+        else:
+            ag_finish(event - STAGES, piece, sub)
+            if event == STAGES:
+                opt_do(piece, sub, True, False)
+            if event < 2 * STAGES - 1:
+                ag_start(event - STAGES + 1, piece, sub)
 
     def service(k, point):
-        one, two, three, four = k - 1, k - 2, k - 3, k - 4
-        if point == 0:
-
-            @pl.when(active(one))
-            def _():
-                rs_start(0, one)
-
-            @pl.when(active(three))
-            def _():
-                ag_finish(0, three)
-                ag_start(1, three)
-                opt_do(three, True, False)
-
-            @pl.when(active(two))
-            def _():
-                opt_do(two, False, True)
-
-        if point == 1:
-
-            @pl.when(active(one))
-            def _():
-                rs_finish(0, one)
-                rs_start(1, one)
-
-            @pl.when(active(two))
-            def _():
-                rs_finish(2, two)
-                rs_start(3, two)
-
-            @pl.when(active(three))
-            def _():
-                ag_finish(1, three)
-                ag_start(2, three)
-
-            @pl.when(active(four))
-            def _():
-                ag_finish(3, four)
-                ag_start(4, four)
-
-        if point == 2:
-
-            @pl.when(active(two))
-            def _():
-                rs_finish(3, two)
-                rs_start(4, two)
-
-            @pl.when(active(four))
-            def _():
-                ag_finish(4, four)
-
-        if point == 3:
-
-            @pl.when(active(one))
-            def _():
-                rs_finish(1, one)
-                rs_start(2, one)
-
-            @pl.when(active(two))
-            def _():
-                for half in range(2):
-                    copy = rs_copy(half, STAGES - 1, two % 2)
-                    copy.wait_send()
-                    copy.wait_recv()
-                opt_do(two, False, False)
-                opt_step(two)
-                opt_do(two, True, True)
-                ag_start(0, two)
-
-            @pl.when(active(three))
-            def _():
-                ag_finish(2, three)
-                ag_start(3, three)
+        due = [(event - 1, sub, at) for sub in range(SUBS) for event, at in enumerate(TIMES[sub]) if at % 4 == point]
+        for event, sub, at in sorted(due, key=lambda one: (-one[0], -one[2], one[1])):
+            piece = k - at // 4
+
+            @pl.when(jnp.logical_and(piece >= 0, piece < PIECES))
+            def _(event=event, piece=piece, sub=sub):
+                go_on(event, piece, sub)
 
     def w_copy(which, piece):
         layer, at_cols = layer_of(piece), pl.ds(pl.multiple_of(chunk_of(piece) * c, c), c)
@@ -374,7 +332,7 @@
             p_copy(piece, tile).start()
 
     def weight_part(which, piece):
-        grads, to = (dg, du)[which], (ga, gb)[which]
+        grads = (dg, du)[which]
 
         @pl.when(layer_of(piece) == 1)
         def _():
@@ -398,11 +356,13 @@
             if which == 1:
                 w_copy(2, following).start()
 
-        n = c // 2
-        for j in range(2):
-            term = dot(at[...], grads[:, j * n : (j + 1) * n])
+        for which_, (grads_, to) in enumerate(((dg, ga), (du, gb))):
+            n = c // 2
+            term = dot(at[...], grads_[:, which * n : (which + 1) * n])
             for i in range(32):
-                to[piece % 2, place(i, ORDERS[which]), :, j * n : (j + 1) * n] = term[i * r : (i + 1) * r, :].astype(BF)
+                for sub in range(SUBS // 2):
+                    block = term[i * r : (i + 1) * r, sub * e : (sub + 1) * e].astype(BF)
+                    to[piece % 2, which * (SUBS // 2) + sub, place(i, ORDERS[which_])] = block
 
     def tile_copy(piece, tile, source):
         return pltpu.make_async_copy(source.at[:, pl.ds(tile * wide, wide)], (dg, du)[tile % 2].at[:, pl.ds(0, wide)], load_sem.at[tile % 2])
@@ -422,9 +382,9 @@
         term = dot(dht[at_rows, :], (dg, du)[tile % 2][:, :wide]).T
         for i in range(4):
             for j in range(8):
-                half, jj = j // 4, j % 4
+                half, sub = j // SUBS, j % SUBS
                 block = term[(8 * i + j) * r : (8 * i + j + 1) * r, :].astype(BF)
-                g_bufs[half][piece % 2, place(4 * tile + i, ORDERS[half]), :, jj * e : (jj + 1) * e] = block
+                g_bufs[half][piece % 2, sub, place(4 * tile + i, ORDERS[half])] = block
         if tile + 2 < 8:
             tile_start(piece, tile + 2)
 
@@ -533,7 +493,7 @@
 
         return 0
 
-    lax.fori_loop(0, PIECES + 4, tick, 0)
+    lax.fori_loop(0, TICKS, tick, 0)
 
 
 def train_step(x, dy, h, p0, weights, ms, vs):
@@ -542,24 +502,23 @@
     c, r, e = ff // CHUNKS, d // 32, d // PARTS
     rows = min(512, tokens // 4)
     any_ = pl.BlockSpec(memory_space=pl.ANY)
-    blocks = lambda *n: pltpu.VMEM((*n, r, c), BF)
+    blocks = lambda *n: pltpu.VMEM((*n, r, e), BF)
     scratch = [
         pltpu.VMEM((tokens, d), BF), pltpu.VMEM((d, tokens), BF), pltpu.VMEM((tokens, d), BF), pltpu.VMEM((d, tokens), BF),
         pltpu.VMEM((d, c), BF), pltpu.VMEM((d, c), BF), pltpu.VMEM((c, d), BF),
         pltpu.VMEM((tokens, c), BF), pltpu.VMEM((tokens, c), BF),
         pltpu.VMEM((2, rows, c), BF),
         pltpu.VMEM((tokens, d), F32),
-        blocks(2, 32), blocks(2, 32),
-        *[blocks(2, 16 >> s) for s in range(STAGES)] * 2,
-        *[blocks(16 >> s) for s in range(STAGES - 1)] * 2,
-        blocks(2), pltpu.VMEM((2, r, c), F32), pltpu.VMEM((2, r, c), F32), blocks(2),
-        pltpu.VMEM((2, 4 * r, e), F32), pltpu.VMEM((2, 4 * r, e), F32), pltpu.VMEM((2, 4 * r, e), BF),
-        pltpu.SemaphoreType.DMA((2, STAGES)), pltpu.SemaphoreType.DMA((2, STAGES, 2)),
-        pltpu.SemaphoreType.DMA((2, STAGES)), pltpu.SemaphoreType.DMA((2, STAGES, 2)),
-        pltpu.SemaphoreType.DMA((2,)), pltpu.SemaphoreType.DMA((4,)), pltpu.SemaphoreType.DMA((3,)), pltpu.SemaphoreType.DMA((2,)),
-        pltpu.SemaphoreType.DMA((2, 3)),
+        blocks(2, SUBS, 32), blocks(2, SUBS, 32),
+        *[blocks(2, SUBS, 16 >> s) for s in range(STAGES)] * 2,
+        *[blocks(SUBS, 16 >> s) for s in range(STAGES - 1)] * 2,
+        blocks(2, SUBS), pltpu.VMEM((2, SUBS, r, e), F32), pltpu.VMEM((2, SUBS, r, e), F32), blocks(2, SUBS),
+        pltpu.SemaphoreType.DMA((2, STAGES, SUBS)), pltpu.SemaphoreType.DMA((2, STAGES, SUBS, 2)),
+        pltpu.SemaphoreType.DMA((2, STAGES, SUBS)), pltpu.SemaphoreType.DMA((2, STAGES, SUBS, 2)),
+        pltpu.SemaphoreType.DMA((2, SUBS)), pltpu.SemaphoreType.DMA((4,)), pltpu.SemaphoreType.DMA((3,)), pltpu.SemaphoreType.DMA((2,)),
+        pltpu.SemaphoreType.DMA((2, 3, SUBS)),
     ]
-    packed = jax.ShapeDtypeStruct((PIECES, 32, r, c), BF)
+    packed = jax.ShapeDtypeStruct((PIECES, SUBS, 32, r, e), BF)
     like = [jax.ShapeDtypeStruct(t.shape, F32) for t in (*ms, *vs)]
     return pl.pallas_call(
         step_kernel,
@@ -573,50 +532,53 @@
     )(x, dy, h, p0, *weights, *ms, *vs)
 
 
-def unpack_kernel(gate_ref, up_ref, down_a, down_b, wg_ref, wu_ref, wd_ref):
-    r, c = gate_ref.shape[-2:]
-    e = c // 4
+def unpack_kernel(gate_ref, up_ref, down_a, down_b, *refs):
+    r, e = gate_ref.shape[-2:]
+    moments, (wg_ref, wu_ref, wd_ref), moments_out = refs[:6], refs[6:9], refs[9:]
+    for source, to in zip(moments, moments_out, strict=True):
+        to[...] = source[...]
     for core in range(2):
         for z0 in range(2):
             for z1 in range(2):
                 owner = z1 * 4 + z0 * 2 + core
-                for chunk in range(CHUNKS):
-                    at_cols = pl.ds(chunk * c, c)
-                    wg_ref[pl.ds(owner * r, r), at_cols] = gate_ref[chunk, core, z0, z1]
-                    wu_ref[pl.ds(owner * r, r), at_cols] = up_ref[chunk, core, z0, z1]
-                for part in range(PARTS):
-                    for half, ref in enumerate((down_a, down_b)):
-                        for j in range(4):
-                            at_rows = pl.ds(owner * 8 * r + (half * 4 + j) * r, r)
-                            wd_ref[at_rows, pl.ds(part * e, e)] = ref[part, core, z0, z1, :, pl.ds(j * e, e)]
-
-
-def unpack(wa, wb, d, ff):
-    r, c = wa.shape[-2:]
-    wa, wb = (t.reshape(PIECES, *(2,) * 5, r, c) for t in (wa, wb))
-    block = (None, 2, None, 2, r, c)
+                for sub in range(SUBS):
+                    for chunk in range(CHUNKS):
+                        at_rows, at_cols = pl.ds(owner * r, r), pl.ds((chunk * SUBS + sub) * e, e)
+                        wg_ref[at_rows, at_cols] = gate_ref[chunk, sub, core, z0, z1]
+                        wu_ref[at_rows, at_cols] = up_ref[chunk, sub, core, z0, z1]
+                    for part in range(PARTS):
+                        for half, ref in enumerate((down_a, down_b)):
+                            at_rows = pl.ds((owner * 8 + half * SUBS + sub) * r, r)
+                            wd_ref[at_rows, pl.ds(part * e, e)] = ref[part, sub, core, z0, z1]
+
+
+def unpack(wa, wb, moments, d, ff):
+    r, e = wa.shape[-2:]
+    wa, wb = (t.reshape(PIECES, SUBS, *(2,) * 5, r, e) for t in (wa, wb))
 
     def spec(n, first, half):
         def index(layer, x, y):
             outer, inner = (x, y) if half == 0 else (y, x)
-            return (first(layer), 0, outer, 0, inner, 0, 0, 0)
-
-        return pl.BlockSpec((n, 2, None, 2, None, 2, r, c), index)
+            return (first(layer), 0, 0, outer, 0, inner, 0, 0, 0)
+
+        return pl.BlockSpec((n, SUBS, 2, None, 2, None, 2, r, e), index)
 
     wide, part = lambda layer: 2 - 2 * layer, lambda layer: 3 - layer
+    slab = lambda rows, cols: pl.BlockSpec((None, rows, cols), lambda layer, x, y: (layer, 2 * x + y, 0))
+    moment = [
+        pl.BlockSpec((None, r, ff // 4), lambda layer, x, y: (layer, 0, 2 * x + y)) if t.shape[2] == ff else slab(2 * r, d) for t in moments
+    ]
     return pl.pallas_call(
         unpack_kernel,
         name="unpack",
         grid=(2, 2, 2),
-        in_specs=[spec(CHUNKS, wide, 0), spec(CHUNKS, wide, 1), spec(PARTS, part, 0), spec(PARTS, part, 1)],
-        out_specs=[
-            pl.BlockSpec((None, d // 4, ff), lambda layer, x, y: (layer, 2 * x + y, 0)),
-            pl.BlockSpec((None, d // 4, ff), lambda layer, x, y: (layer, 2 * x + y, 0)),
-            pl.BlockSpec((None, ff // 4, d), lambda layer, x, y: (layer, 2 * x + y, 0)),
-        ],
-        out_shape=[jax.ShapeDtypeStruct((2, d, ff), BF)] * 2 + [jax.ShapeDtypeStruct((2, ff, d), BF)],
+        in_specs=[spec(CHUNKS, wide, 0), spec(CHUNKS, wide, 1), spec(PARTS, part, 0), spec(PARTS, part, 1), *moment],
+        out_specs=[slab(d // 4, ff), slab(d // 4, ff), slab(ff // 4, d), *moment],
+        out_shape=[jax.ShapeDtypeStruct((2, d, ff), BF)] * 2
+        + [jax.ShapeDtypeStruct((2, ff, d), BF)]
+        + [jax.ShapeDtypeStruct(t.shape, F32) for t in moments],
         compiler_params=pltpu.CompilerParams(vmem_limit_bytes=60 << 20),
-    )(wa, wb, wa, wb)
+    )(wa, wb, wa, wb, *moments)
 
 
 def solution(mesh):
@@ -626,7 +588,7 @@
         x, dy = x[0], dy[0]
         p0, h = forward(x, wg, wu, wd, 0)
         wa, wb, *moments, _ = train_step(x, dy, h, p0, (wg, wu, wd), ms, vs)
-        return (*unpack(wa, wb, x.shape[1], wg.shape[2]), *moments)
+        return tuple(unpack(wa, wb, moments, x.shape[1], wg.shape[2]))
 
     seq, whole, rows = P(("rep", "dp")), P(), P(None, "dp")
     return jax.shard_map(

time: 761 us -> 656 us (0.86)
  Pallas kernels: 750 us -> 655 us
  local copies, waits for them, and re-layouts: 9.49 us -> 0 us
    pallas_call x1, Pallas kernels: 637 us -> 538 us  [train_step(): pl.pallas_call(step_kernel, name='step', in_specs=[any_] * 13, out_specs=...]
    unnamed x18 -> x0, local copies, waits for them, and re-layouts: 9.49 us -> none
where the time goes in v3:
time: 656 us; the launch traced here: 655 us
  Pallas kernels  655 us (100%)
    pallas_call x1, Pallas kernels, train_step(): pl.pallas_call(step_kernel, name='step', in_specs=[any_] * 13, out_specs=...  538 us
    pallas_call x1, Pallas kernels, forward(): pl.pallas_call(forward_kernel, name='forward', grid=(CHUNKS, tokens // ro...  76.3 us
    pallas_call x1, Pallas kernels, unpack(): pl.pallas_call(unpack_kernel, name='unpack', grid=(2, 2, 2), in_specs=[sp...  40.8 us

profile of v3, /device:TPU:0, one launch (start us, length us, event | category | flops | bytes accessed | tf_op | source)
XLA Modules:
  0.0 655.4 jit_solution(13569621158066639443)
XLA Ops:
  0.6 76.3 %forward.1 = (bf16[2048,6144]{1,0:T(8,128)(2,1)}, bf16[2048,768]{1,0:T(8,128)(2,1)}) custom-call(bf16[2048,768]{1,0:T(8,128)(2,1)} %bitcast.8, bf16[2,768,6144]{2,1,0:T(8,128)(2,1)} %wg_hbm.1, bf16[2,768,6144]{2,1,0:T(8,128)(2,1)} %wu_hbm.1, bf16[2,6144,768]{2,1,0:T(8,128)(2,1)} %wd_hbm.1), custom_call_target="tpu_custom_call" | custom-call | flops 57982058496 | bytes 62914560 | tf_op jit(solution)/shard_map/forward/pallas_call | solution.py:95
  76.9 537.5 %step.1 = (bf16[18,4,32,24,256]{4,3,2,1,0:T(8,128)(2,1)}, bf16[18,4,32,24,256]{4,3,2,1,0:T(8,128)(2,1)}, f32[2,24,6144]{2,1,0:T(8,128)}, f32[2,24,6144]{2,1,0:T(...) custom-call(bf16[2048,768]{1,0:T(8,128)(2,1)} %bitcast.9, ...), custom_call_target="tpu_custom_call" | custom-call | flops 270582939648 | bytes 419430400 | tf_op jit(solution)/shard_map/step/pallas_call | solution.py:523
  614.5 40.8 %unpack.1 = (bf16[2,768,6144]{2,1,0:T(8,128)(2,1)}, bf16[2,768,6144]{2,1,0:T(8,128)(2,1)}, bf16[2,6144,768]{2,1,0:T(8,128)(2,1)}, f32[2,24,6144]{2,1,0:T(8,128)}...) custom-call(bf16[18,4,2,2,2,2,2,24,256]{8,7,6,5,4,3,2,1,0:T(8,128)(2, ...), custom_call_target="tpu_custom_call" | custom-call | tf_op jit(solution)/shard_map/unpack/pallas_call | solution.py:571

commit v4 on v3

--- a/solution.py
+++ b/solution.py
@@ -19,14 +19,16 @@
 PARTS = 3
 PIECES = 2 * (CHUNKS + PARTS)
 FRONT = 4
+STRIP = 32
 SUBS = 4
+POINTS = 8
 TIMES = (
-    (4, 5, 7, 9, 11, 12, 13, 14, 16, 19, 23),
-    (5, 6, 8, 10, 11, 12, 13, 17, 20, 23, 27),
-    (4, 7, 9, 11, 12, 13, 14, 15, 17, 20, 24),
-    (6, 8, 10, 12, 13, 14, 15, 16, 19, 22, 24),
+    (8, 10, 15, 19, 21, 24, 26, 30, 35, 42, 49),
+    (10, 14, 18, 22, 24, 26, 29, 33, 39, 46, 49),
+    (11, 16, 22, 26, 29, 31, 33, 40, 45, 52, 58),
+    (9, 11, 19, 23, 25, 27, 31, 36, 41, 48, 56),
 )
-TICKS = PIECES + max(t[-1] for t in TIMES) // 4
+TICKS = PIECES + max(t[-1] for t in TIMES) // POINTS
 
 
 def dot(a, b, dims=NN):
@@ -112,12 +114,12 @@
 
 def step_kernel(
     x_hbm, dy_hbm, h_hbm, p0_hbm, wg_hbm, wu_hbm, wd_hbm, mg_hbm, mu_hbm, md_hbm, vg_hbm, vu_hbm, vd_hbm,
-    wa_out, wb_out, mg_out, mu_out, md_out, vg_out, vu_out, vd_out, p1_hbm,
+    wa_out, wb_out, mg_out, mu_out, md_out, vg_out, vu_out, vd_out, p1_hbm, dg_hbm, du_hbm,
     a, at, dh, dht, wg, wu, wd, dg, du, ps, da, ga, gb, *rest,
 ):
     (ra, rb, sa, sb), rest = (rest[0:5], rest[5:10], rest[10:14], rest[14:18]), rest[18:]
     wn, mo, vo, wo, *rest = rest
-    rs_send, rs_recv, ag_send, ag_recv, own_sem, load_sem, w_sem, p_sem, opt_sem = rest
+    rs_send, rs_recv, ag_send, ag_recv, own_sem, load_sem, w_sem, p_sem, opt_sem, d_sem = rest
 
     tokens, d = a.shape
     c = wg.shape[1]
@@ -290,16 +292,16 @@
                 ag_start(event - STAGES + 1, piece, sub)
 
     def service(k, point):
-        due = [(event - 1, sub, at) for sub in range(SUBS) for event, at in enumerate(TIMES[sub]) if at % 4 == point]
+        due = [(event - 1, sub, at) for sub in range(SUBS) for event, at in enumerate(TIMES[sub]) if at % POINTS == point]
         for event, sub, at in sorted(due, key=lambda one: (-one[0], -one[2], one[1])):
-            piece = k - at // 4
+            piece = k - at // POINTS
 
             @pl.when(jnp.logical_and(piece >= 0, piece < PIECES))
             def _(event=event, piece=piece, sub=sub):
                 go_on(event, piece, sub)
 
-    def w_copy(which, piece):
-        layer, at_cols = layer_of(piece), pl.ds(pl.multiple_of(chunk_of(piece) * c, c), c)
+    def w_copy(which, layer, chunk):
+        at_cols = pl.ds(pl.multiple_of(chunk * c, c), c)
         if which == 2:
             return pltpu.make_async_copy(wd_hbm.at[layer, at_cols, :], wd, w_sem.at[2])
         return pltpu.make_async_copy((wg_hbm, wu_hbm)[which].at[layer, :, at_cols], (wg, wu)[which], w_sem.at[which])
@@ -309,6 +311,11 @@
         at_cols = pl.ds(pl.multiple_of(chunk_of(piece) * c, c), c)
         return pltpu.make_async_copy(ps.at[slot], p1_hbm.at[pl.ds(pl.multiple_of(tile * rows, rows), rows), at_cols], p_sem.at[slot])
 
+    def d_copy(which, chunk, tile, load):
+        here = pl.ds(pl.multiple_of(tile * rows, rows), rows)
+        vmem, hbm = (dg, du)[which].at[here, :], (dg_hbm, du_hbm)[which].at[here, pl.ds(pl.multiple_of(chunk * c, c), c)]
+        return pltpu.make_async_copy(*((hbm, vmem) if load else (vmem, hbm)), d_sem.at[which, tile])
+
     def front_tile(piece, tile):
         here = pl.ds(pl.multiple_of(tile * rows, rows), rows)
         at_, dh_ = a[here, :], dh[here, :]
@@ -319,50 +326,50 @@
         n = c // FRONT
         for j in range(FRONT):
             cols = slice(j * n, (j + 1) * n)
-            gate, up = dot(at_, wg[:, cols]), dot(at_, wu[:, cols])
-            dp = dot(dh_, wd[cols, :], NT).astype(BF).astype(F32)
-            s = sigmoid(gate)
-            gs = gate * s
-            ps[tile % 2, :, cols] = (gs * up).astype(BF)
-            du[here, cols] = (dp * gs).astype(BF)
-            dg[here, cols] = (dp * up * (s * (1.0 + gate * (1.0 - s)))).astype(BF)
+            gates, ups = dot(at_, wg[:, cols]), dot(at_, wu[:, cols])
+            dps = dot(dh_, wd[cols, :], NT)
+            for i in range(0, rows, STRIP):
+                gate, up = gates[i : i + STRIP], ups[i : i + STRIP]
+                dp = dps[i : i + STRIP].astype(BF).astype(F32)
+                s = sigmoid(gate)
+                gs = gate * s
+                out = pl.ds(pl.multiple_of(tile * rows + i, STRIP), STRIP)
+                ps[tile % 2, i : i + STRIP, cols] = (gs * up).astype(BF)
+                du[out, cols] = (dp * gs).astype(BF)
+                dg[out, cols] = (dp * up * (s + gs * (1.0 - s))).astype(BF)
 
         @pl.when(layer_of(piece) == 1)
         def _():
             p_copy(piece, tile).start()
-
-    def weight_part(which, piece):
-        grads = (dg, du)[which]
-
-        @pl.when(layer_of(piece) == 1)
-        def _():
-            def back(tile, _):
-                here = pl.ds(pl.multiple_of(tile * rows, rows), rows)
-                part = dot(grads[here, :], (wg, wu)[which][...], NT)
-                if which == 0:
-                    old = jnp.where(chunk_of(piece) == 0, jnp.zeros_like(part), da[here, :])
-                    da[here, :] = old + part
-                else:
-                    da[here, :] += part
-                return 0
-
-            lax.fori_loop(0, tiles, back, 0)
-
-        following = jnp.where(piece < CHUNKS - 1, piece + 1, jnp.where(piece < CHUNKS, CHUNKS + 2 * PARTS, piece + 1))
-
-        @pl.when(following < PIECES)
-        def _():
-            w_copy(which, following).start()
-            if which == 1:
-                w_copy(2, following).start()
-
-        for which_, (grads_, to) in enumerate(((dg, ga), (du, gb))):
-            n = c // 2
-            term = dot(at[...], grads_[:, which * n : (which + 1) * n])
-            for i in range(32):
-                for sub in range(SUBS // 2):
-                    block = term[i * r : (i + 1) * r, sub * e : (sub + 1) * e].astype(BF)
-                    to[piece % 2, which * (SUBS // 2) + sub, place(i, ORDERS[which_])] = block
+            for which in range(2):
+                d_copy(which, chunk_of(piece), tile, False).start()
+
+    def weight_part(side, which, piece):
+        n = c // 2
+        term = dot(at[...], (dg, du)[which][:, side * n : (side + 1) * n])
+        for i in range(32):
+            for sub in range(SUBS // 2):
+                block = term[i * r : (i + 1) * r, sub * e : (sub + 1) * e].astype(BF)
+                (ga, gb)[which][piece % 2, side * (SUBS // 2) + sub, place(i, ORDERS[which])] = block
+
+    def through_layer(which, chunk, more):
+        w_copy(which, 1, chunk).wait()
+
+        def back(tile, _):
+            here = pl.ds(pl.multiple_of(tile * rows, rows), rows)
+            d_copy(which, chunk, tile, True).wait()
+            part = dot((dg, du)[which][here, :], (wg, wu)[which][...], NT)
+            if which == 0:
+                da[here, :] = jnp.where(chunk == 0, jnp.zeros_like(part), da[here, :]) + part
+            else:
+                da[here, :] += part
+            if more:
+                d_copy(which, chunk + 1, tile, True).start()
+            return 0
+
+        lax.fori_loop(0, tiles, back, 0)
+        if more:
+            w_copy(which, 1, chunk + 1).start()
 
     def tile_copy(piece, tile, source):
         return pltpu.make_async_copy(source.at[:, pl.ds(tile * wide, wide)], (dg, du)[tile % 2].at[:, pl.ds(0, wide)], load_sem.at[tile % 2])
@@ -431,7 +438,7 @@
     first = (
         pltpu.make_async_copy(h_hbm, a, load_sem.at[2]),
         pltpu.make_async_copy(dy_hbm, dh, load_sem.at[3]),
-        *(w_copy(which, 0) for which in range(3)),
+        *(w_copy(which, 1, 0) for which in range(3)),
     )
     for copy in first:
         copy.start()
@@ -445,40 +452,62 @@
         computes = k < PIECES
         gated = jnp.logical_and(computes, is_wide(k))
         downs = jnp.logical_and(computes, jnp.logical_not(is_wide(k)))
+        downs_1 = jnp.logical_and(downs, layer_of(k) == 1)
 
         @pl.when(downs)
         def _():
             tile_start(k, 0)
             tile_start(k, 1)
 
-        for point in range(4):
+        @pl.when(downs_1)
+        def _():
+            for which in range(2):
+                w_copy(which, 1, 2 * part_of(k)).start()
+
+        for point in range(POINTS):
             service(k, point)
 
             @pl.when(gated)
             def _(point=point):
                 if point == 0:
                     for which in range(3):
-                        w_copy(which, k).wait()
-                if point < 2:
-
-                    def front(i, _):
-                        front_tile(k, i + point * (tiles // 2))
-                        return 0
-
-                    lax.fori_loop(0, tiles // 2, front, 0)
+                        w_copy(which, layer_of(k), chunk_of(k)).wait()
+                if point < 4:
+                    front_tile(k, point)
                 else:
-                    weight_part(point - 2, k)
+                    weight_part(point // 2 - 2, point % 2, k)
                 if point == 3:
+                    @pl.when(jnp.logical_and(k != CHUNKS - 1, k < PIECES - 1))
+                    def _():
+                        for which in range(3):
+                            w_copy(which, layer_of(k), chunk_of(k) + 1).start()
+
+                if point == POINTS - 1:
 
                     @pl.when(layer_of(k) == 1)
                     def _():
                         p_copy(k, tiles - 2).wait()
                         p_copy(k, tiles - 1).wait()
-
-            @pl.when(downs)
-            def _(point=point):
-                down_tile(k, 2 * point)
-                down_tile(k, 2 * point + 1)
+                        for which in range(2):
+                            for tile in range(tiles):
+                                d_copy(which, chunk_of(k), tile, False).wait()
+
+            if point < 4:
+
+                @pl.when(downs)
+                def _(point=point):
+                    down_tile(k, 2 * point)
+                    down_tile(k, 2 * point + 1)
+
+            else:
+
+                @pl.when(downs_1)
+                def _(point=point):
+                    if point == 4:
+                        for tile in range(tiles):
+                            for which in range(2):
+                                d_copy(which, 2 * part_of(k), tile, True).start()
+                    through_layer(point % 2, 2 * part_of(k) + point // 2 - 2, point < 6)
 
         @pl.when(k == CHUNKS - 1)
         def _():
@@ -486,6 +515,8 @@
 
         @pl.when(k == CHUNKS + PARTS - 1)
         def _():
+            for which in range(3):
+                w_copy(which, 0, 0).start()
             through_norm()
             turn(dh, dht)
             x_copy.wait()
@@ -516,7 +547,7 @@
         pltpu.SemaphoreType.DMA((2, STAGES, SUBS)), pltpu.SemaphoreType.DMA((2, STAGES, SUBS, 2)),
         pltpu.SemaphoreType.DMA((2, STAGES, SUBS)), pltpu.SemaphoreType.DMA((2, STAGES, SUBS, 2)),
         pltpu.SemaphoreType.DMA((2, SUBS)), pltpu.SemaphoreType.DMA((4,)), pltpu.SemaphoreType.DMA((3,)), pltpu.SemaphoreType.DMA((2,)),
-        pltpu.SemaphoreType.DMA((2, 3, SUBS)),
+        pltpu.SemaphoreType.DMA((2, 3, SUBS)), pltpu.SemaphoreType.DMA((2, 4)),
     ]
     packed = jax.ShapeDtypeStruct((PIECES, SUBS, 32, r, e), BF)
     like = [jax.ShapeDtypeStruct(t.shape, F32) for t in (*ms, *vs)]
@@ -524,8 +555,8 @@
         step_kernel,
         name="step",
         in_specs=[any_] * 13,
-        out_specs=[any_] * 9,
-        out_shape=[packed, packed, *like, jax.ShapeDtypeStruct((tokens, ff), BF)],
+        out_specs=[any_] * 11,
+        out_shape=[packed, packed, *like, *[jax.ShapeDtypeStruct((tokens, ff), BF)] * 3],
         scratch_shapes=scratch,
         compiler_params=pltpu.CompilerParams(collective_id=0, has_side_effects=True, vmem_limit_bytes=67_000_000),
         cost_estimate=pl.CostEstimate(flops=28 * tokens * d * ff, bytes_accessed=400 << 20, transcendentals=0),
@@ -587,7 +618,7 @@
         ms, vs = arrays[3:6], arrays[6:9]
         x, dy = x[0], dy[0]
         p0, h = forward(x, wg, wu, wd, 0)
-        wa, wb, *moments, _ = train_step(x, dy, h, p0, (wg, wu, wd), ms, vs)
+        wa, wb, *moments, _, _, _ = train_step(x, dy, h, p0, (wg, wu, wd), ms, vs)
         return tuple(unpack(wa, wb, moments, x.shape[1], wg.shape[2]))
 
     seq, whole, rows = P(("rep", "dp")), P(), P(None, "dp")

time: 656 us -> 653 us (level)
  no operation moved by 1% of the time
where the time goes in v4:
time: 653 us; the launch traced here: 652 us
  Pallas kernels  651 us (100%)
    pallas_call x1, Pallas kernels, train_step(): pl.pallas_call(step_kernel, name='step', in_specs=[any_] * 13, out_specs=...  534 us
    pallas_call x1, Pallas kernels, forward(): pl.pallas_call(forward_kernel, name='forward', grid=(CHUNKS, tokens // ro...  76.3 us
    pallas_call x1, Pallas kernels, unpack(): pl.pallas_call(unpack_kernel, name='unpack', grid=(2, 2, 2), in_specs=[sp...  40.8 us

profile of v4, /device:TPU:0, one launch (start us, length us, event | category | flops | bytes accessed | tf_op | source)
XLA Modules:
  0.0 652.1 jit_solution(1342109640792088445)
XLA Ops:
  0.6 76.3 %forward.1 = (bf16[2048,6144]{1,0:T(8,128)(2,1)}, bf16[2048,768]{1,0:T(8,128)(2,1)}) custom-call(bf16[2048,768]{1,0:T(8,128)(2,1)} %bitcast.8, bf16[2,768,6144]{2,1,0:T(8,128)(2,1)} %wg_hbm.1, bf16[2,768,6144]{2,1,0:T(8,128)(2,1)} %wu_hbm.1, bf16[2,6144,768]{2,1,0:T(8,128)(2,1)} %wd_hbm.1), custom_call_target="tpu_custom_call" | custom-call | flops 57982058496 | bytes 62914560 | tf_op jit(solution)/shard_map/forward/pallas_call | solution.py:97
  76.9 534.3 %step.1 = (bf16[18,4,32,24,256]{4,3,2,1,0:T(8,128)(2,1)}, bf16[18,4,32,24,256]{4,3,2,1,0:T(8,128)(2,1)}, f32[2,24,6144]{2,1,0:T(8,128)}, f32[2,24,6144]{2,1,0:T(...) custom-call(bf16[2048,768]{1,0:T(8,128)(2,1)} %bitcast.9, ...), custom_call_target="tpu_custom_call" | custom-call | flops 270582939648 | bytes 419430400 | tf_op jit(solution)/shard_map/step/pallas_call | solution.py:554
  611.2 40.8 %unpack.1 = (bf16[2,768,6144]{2,1,0:T(8,128)(2,1)}, bf16[2,768,6144]{2,1,0:T(8,128)(2,1)}, bf16[2,6144,768]{2,1,0:T(8,128)(2,1)}, f32[2,24,6144]{2,1,0:T(8,128)}...) custom-call(bf16[18,4,2,2,2,2,2,24,256]{8,7,6,5,4,3,2,1,0:T(8,128)(2, ...), custom_call_target="tpu_custom_call" | custom-call | tf_op jit(solution)/shard_map/unpack/pallas_call | solution.py:602

commit v5 on v4

--- a/solution.py
+++ b/solution.py
@@ -20,13 +20,12 @@
 PIECES = 2 * (CHUNKS + PARTS)
 FRONT = 4
 STRIP = 32
-SUBS = 4
+SUBS = 2
+GROUPS = 4 // SUBS
 POINTS = 8
 TIMES = (
-    (8, 10, 15, 19, 21, 24, 26, 30, 35, 42, 49),
-    (10, 14, 18, 22, 24, 26, 29, 33, 39, 46, 49),
-    (11, 16, 22, 26, 29, 31, 33, 40, 45, 52, 58),
-    (9, 11, 19, 23, 25, 27, 31, 36, 41, 48, 56),
+    (8, 9, 13, 17, 20, 24, 28, 31, 38, 44, 48),
+    (10, 11, 15, 21, 23, 26, 31, 35, 40, 47, 55),
 )
 TICKS = PIECES + max(t[-1] for t in TIMES) // POINTS
 
@@ -62,7 +61,7 @@
     return (w - 0.02 * step).astype(BF), m, v
 
 
-def forward_kernel(x_ref, wg_ref, wu_ref, wd_ref, p_ref, h_ref, a_all, total):
+def forward_kernel(x_ref, wg_ref, wu_ref, wd_ref, p_ref, h_ref, gate_ref, up_ref, a_all, total):
     chunk, tile = pl.program_id(0), pl.program_id(1)
     rows = p_ref.shape[0]
     here = pl.ds(pl.multiple_of(tile * rows, rows), rows)
@@ -73,6 +72,7 @@
 
     a = a_all[here, :]
     gate, up = dot(a, wg_ref[...]), dot(a, wu_ref[...])
+    gate_ref[...], up_ref[...] = gate, up
     p = (gate * sigmoid(gate) * up).astype(BF)
     p_ref[...] = p
 
@@ -104,8 +104,16 @@
             pl.BlockSpec((None, d, c), lambda i, t: (layer, 0, i)),
             pl.BlockSpec((None, c, d), lambda i, t: (layer, i, 0)),
         ],
-        out_specs=[pl.BlockSpec((rows, c), lambda i, t: (t, i)), pl.BlockSpec((tokens, d), lambda i, t: (0, 0))],
-        out_shape=[jax.ShapeDtypeStruct((tokens, ff), BF), jax.ShapeDtypeStruct((tokens, d), BF)],
+        out_specs=[
+            pl.BlockSpec((rows, c), lambda i, t: (t, i)),
+            pl.BlockSpec((tokens, d), lambda i, t: (0, 0)),
+            *[pl.BlockSpec((rows, c), lambda i, t: (t, i))] * 2,
+        ],
+        out_shape=[
+            jax.ShapeDtypeStruct((tokens, ff), BF),
+            jax.ShapeDtypeStruct((tokens, d), BF),
+            *[jax.ShapeDtypeStruct((tokens, ff), F32)] * 2,
+        ],
         scratch_shapes=[pltpu.VMEM((tokens, d), BF), pltpu.VMEM((tokens, d), F32)],
         compiler_params=pltpu.CompilerParams(vmem_limit_bytes=60 << 20),
         cost_estimate=pl.CostEstimate(flops=6 * tokens * d * ff, bytes_accessed=60 << 20, transcendentals=0),
@@ -113,13 +121,13 @@
 
 
 def step_kernel(
-    x_hbm, dy_hbm, h_hbm, p0_hbm, wg_hbm, wu_hbm, wd_hbm, mg_hbm, mu_hbm, md_hbm, vg_hbm, vu_hbm, vd_hbm,
+    x_hbm, dy_hbm, h_hbm, p0_hbm, gate_hbm, up_hbm, wg_hbm, wu_hbm, wd_hbm, mg_hbm, mu_hbm, md_hbm, vg_hbm, vu_hbm, vd_hbm,
     wa_out, wb_out, mg_out, mu_out, md_out, vg_out, vu_out, vd_out, p1_hbm, dg_hbm, du_hbm,
-    a, at, dh, dht, wg, wu, wd, dg, du, ps, da, ga, gb, *rest,
+    a, at, dh, dht, wg, wu, wd, dg, du, ps, big, ga, gb, *rest,
 ):
     (ra, rb, sa, sb), rest = (rest[0:5], rest[5:10], rest[10:14], rest[14:18]), rest[18:]
     wn, mo, vo, wo, *rest = rest
-    rs_send, rs_recv, ag_send, ag_recv, own_sem, load_sem, w_sem, p_sem, opt_sem, d_sem = rest
+    rs_send, rs_recv, ag_send, ag_recv, own_sem, load_sem, w_sem, p_sem, opt_sem, d_sem, gu_sem = rest
 
     tokens, d = a.shape
     c = wg.shape[1]
@@ -163,7 +171,7 @@
 
     def rs_add(stage, piece, sub):
         n = 16 >> stage
-        some = min(n, 4)
+        some = min(n, SUBS)
         for half in range(2):
             own = bit_of(me, ORDERS[half][stage])
             source = g_bufs[half].at[piece % 2, sub] if stage == 0 else s_bufs[half][stage - 1].at[sub]
@@ -229,33 +237,36 @@
 
     def opt_do(piece, sub, out, start):
         layer = layer_of(piece)
-        wide_cols = pl.ds(pl.multiple_of(chunk_of(piece) * c + sub * e, e), e)
         part_cols = pl.ds(pl.multiple_of(part_of(piece) * e, e), e)
 
         def copies(wide):
             for half in range(2):
-                group = (half * SUBS + sub) * r
-                rows_, cols = (slice(None), wide_cols) if wide else (pl.ds(group, r), part_cols)
-                kinds = ((mg_hbm, mu_hbm)[half], mg_out if half == 0 else mu_out, mo), ((vg_hbm, vu_hbm)[half], vg_out if half == 0 else vu_out, vo)
-                if not wide:
-                    kinds = (md_hbm, md_out, mo), (vd_hbm, vd_out, vo)
-                for k, (hbm, hbm_out, vmem) in enumerate(kinds):
-                    sem = opt_sem.at[half, k, sub]
-                    if out:
-                        yield pltpu.make_async_copy(vmem.at[half, sub], hbm_out.at[layer, rows_, cols], sem)
+                for q in range(GROUPS):
+                    group = sub * GROUPS + q
+                    wide_cols = pl.ds(pl.multiple_of(chunk_of(piece) * c + group * e, e), e)
+                    row = (half * 4 + group) * r
+                    rows_, cols = (slice(None), wide_cols) if wide else (pl.ds(row, r), part_cols)
+                    if wide:
+                        kinds = ((mg_hbm, mu_hbm)[half], (mg_out, mu_out)[half], mo), ((vg_hbm, vu_hbm)[half], (vg_out, vu_out)[half], vo)
                     else:
-                        yield pltpu.make_async_copy(hbm.at[layer, rows_, cols], vmem.at[half, sub], sem)
-                if not out:
-                    own = me * r if wide else me * 8 * r + group
-                    source = (wg_hbm, wu_hbm)[half] if wide else wd_hbm
-                    own = pl.ds(pl.multiple_of(own, 8), r)
-                    yield pltpu.make_async_copy(source.at[layer, own, cols], wo.at[half, sub], opt_sem.at[half, 2, sub])
+                        kinds = (md_hbm, md_out, mo), (vd_hbm, vd_out, vo)
+                    for k, (hbm, hbm_out, vmem) in enumerate(kinds):
+                        sem = opt_sem.at[half, k, group]
+                        if out:
+                            yield pltpu.make_async_copy(vmem.at[half, sub, q], hbm_out.at[layer, rows_, cols], sem)
+                        else:
+                            yield pltpu.make_async_copy(hbm.at[layer, rows_, cols], vmem.at[half, sub, q], sem)
+                    if not out:
+                        own = pl.ds(pl.multiple_of(me * r if wide else me * 8 * r + row, 8), r)
+                        source = (wg_hbm, wu_hbm)[half] if wide else wd_hbm
+                        yield pltpu.make_async_copy(source.at[layer, own, cols], wo.at[half, sub, q], opt_sem.at[half, 2, group])
 
         if not start:
             for half in range(2):
-                for k, vmem in enumerate((mo, vo, wo)[: 2 if out else 3]):
-                    block = (mg_hbm, vg_hbm, wg_hbm)[k].at[0, pl.ds(0, r), pl.ds(0, e)]
-                    pltpu.make_async_copy(block, vmem.at[half, sub], opt_sem.at[half, k, sub]).wait()
+                for q in range(GROUPS):
+                    for k, vmem in enumerate((mo, vo, wo)[: 2 if out else 3]):
+                        block = (mg_hbm, vg_hbm, wg_hbm)[k].at[0, pl.ds(0, r), pl.ds(0, e)]
+                        pltpu.make_async_copy(block, vmem.at[half, sub, q], opt_sem.at[half, k, sub * GROUPS + q]).wait()
             return
         for wide in (True, False):
 
@@ -319,7 +330,8 @@
     def front_tile(piece, tile):
         here = pl.ds(pl.multiple_of(tile * rows, rows), rows)
         at_, dh_ = a[here, :], dh[here, :]
-        @pl.when(jnp.logical_and(layer_of(piece) == 1, tile >= 2))
+
+        @pl.when(tile >= 2)
         def _():
             p_copy(piece, tile - 2).wait()
 
@@ -338,62 +350,100 @@
                 du[out, cols] = (dp * gs).astype(BF)
                 dg[out, cols] = (dp * up * (s + gs * (1.0 - s))).astype(BF)
 
-        @pl.when(layer_of(piece) == 1)
-        def _():
-            p_copy(piece, tile).start()
+        p_copy(piece, tile).start()
+        for which in range(2):
+            d_copy(which, chunk_of(piece), tile, False).start()
+
+    def gu_copy(which, chunk, tile):
+        slot = 2 * (tile % 2) + which
+        source = (gate_hbm, up_hbm)[which].at[pl.ds(pl.multiple_of(tile * rows, rows), rows), pl.ds(pl.multiple_of(chunk * c, c), c)]
+        return pltpu.make_async_copy(source, big.at[:, pl.ds(pl.multiple_of(slot * c, c), c)], gu_sem.at[slot])
+
+    def kept_tile(piece, tile):
+        here = pl.ds(pl.multiple_of(tile * rows, rows), rows)
+        dh_ = dh[here, :]
+        for which in range(2):
+            gu_copy(which, chunk_of(piece), tile).wait()
+        n = c // FRONT
+        for j in range(FRONT):
+            cols = slice(j * n, (j + 1) * n)
+            dps = dot(dh_, wd[cols, :], NT)
+            at_gate, at_up = (pl.ds(pl.multiple_of((2 * (tile % 2) + which) * c + j * n, n), n) for which in range(2))
+            for i in range(0, rows, STRIP):
+                gate, up = big[i : i + STRIP, at_gate], big[i : i + STRIP, at_up]
+                dp = dps[i : i + STRIP].astype(BF).astype(F32)
+                s = sigmoid(gate)
+                gs = gate * s
+                out = pl.ds(pl.multiple_of(tile * rows + i, STRIP), STRIP)
+                du[out, cols] = (dp * gs).astype(BF)
+                dg[out, cols] = (dp * up * (s + gs * (1.0 - s))).astype(BF)
+
+        following = piece * tiles + tile + 2
+
+        @pl.when(following < PIECES * tiles)
+        def _():
             for which in range(2):
-                d_copy(which, chunk_of(piece), tile, False).start()
+                gu_copy(which, following // tiles - CHUNKS - 2 * PARTS, following % tiles).start()
 
     def weight_part(side, which, piece):
         n = c // 2
-        term = dot(at[...], (dg, du)[which][:, side * n : (side + 1) * n])
+        term = dot(at[...], (dg, du)[which][:, pl.ds(pl.multiple_of(side * n, n), n)])
         for i in range(32):
-            for sub in range(SUBS // 2):
-                block = term[i * r : (i + 1) * r, sub * e : (sub + 1) * e].astype(BF)
-                (ga, gb)[which][piece % 2, side * (SUBS // 2) + sub, place(i, ORDERS[which])] = block
-
-    def through_layer(which, chunk, more):
+            for q in range(2):
+                group = side * 2 + q
+                block = term[i * r : (i + 1) * r, q * e : (q + 1) * e].astype(BF)
+                (ga, gb)[which][piece % 2, group // GROUPS, place(i, ORDERS[which]), group % GROUPS] = block
+
+    def through_layer(which, piece, side):
+        chunk = 2 * part_of(piece) + side
         w_copy(which, 1, chunk).wait()
 
         def back(tile, _):
             here = pl.ds(pl.multiple_of(tile * rows, rows), rows)
+            total = pl.ds(pl.multiple_of(tile * d, 128), d)
             d_copy(which, chunk, tile, True).wait()
             part = dot((dg, du)[which][here, :], (wg, wu)[which][...], NT)
             if which == 0:
-                da[here, :] = jnp.where(chunk == 0, jnp.zeros_like(part), da[here, :]) + part
+                big[:, total] = jnp.where(chunk == 0, jnp.zeros_like(part), big[:, total]) + part
             else:
-                da[here, :] += part
-            if more:
+                big[:, total] += part
+
+            @pl.when(side == 0)
+            def _():
                 d_copy(which, chunk + 1, tile, True).start()
+
             return 0
 
         lax.fori_loop(0, tiles, back, 0)
-        if more:
+
+        @pl.when(side == 0)
+        def _():
             w_copy(which, 1, chunk + 1).start()
 
-    def tile_copy(piece, tile, source):
-        return pltpu.make_async_copy(source.at[:, pl.ds(tile * wide, wide)], (dg, du)[tile % 2].at[:, pl.ds(0, wide)], load_sem.at[tile % 2])
-
-    def tile_start(piece, tile):
-        @pl.when(layer_of(piece) == 1)
-        def _():
-            tile_copy(piece, tile, p1_hbm).start()
-
-        @pl.when(layer_of(piece) == 0)
-        def _():
-            tile_copy(piece, tile, p0_hbm).start()
-
-    def down_tile(piece, tile):
-        tile_copy(piece, tile, p0_hbm).wait()
+    def tile_copy(which, tile, source):
+        from_cols = pl.ds(pl.multiple_of(tile * wide, 128), wide)
+        return pltpu.make_async_copy(source.at[:, from_cols], (dg, du)[which].at[:, pl.ds(0, wide)], load_sem.at[which])
+
+    def tile_start(piece, which, tile):
+        for layer, source in enumerate((p0_hbm, p1_hbm)):
+
+            @pl.when(layer_of(piece) == layer)
+            def _(source=source):
+                tile_copy(which, tile, source).start()
+
+    def down_tile(piece, which, tile):
+        tile_copy(which, tile, p0_hbm).wait()
         at_rows = pl.ds(pl.multiple_of(part_of(piece) * e, e), e)
-        term = dot(dht[at_rows, :], (dg, du)[tile % 2][:, :wide]).T
+        term = dot(dht[at_rows, :], (dg, du)[which][:, :wide]).T
         for i in range(4):
             for j in range(8):
-                half, sub = j // SUBS, j % SUBS
+                half, group = j // 4, j % 4
                 block = term[(8 * i + j) * r : (8 * i + j + 1) * r, :].astype(BF)
-                g_bufs[half][piece % 2, sub, place(4 * tile + i, ORDERS[half])] = block
-        if tile + 2 < 8:
-            tile_start(piece, tile + 2)
+                g_bufs[half][piece % 2, group // GROUPS, place(4 * tile + i, ORDERS[half]), group % GROUPS] = block
+
+        @pl.when(tile + 2 < 8)
+        def _():
+            tile_start(piece, which, tile + 2)
 
     def through_norm():
         def back(tile, _):
@@ -405,8 +455,9 @@
             def some(i, _):
                 at_rows = pl.ds(pl.multiple_of(i * 32, 32), 32)
                 at_all = pl.ds(pl.multiple_of(tile * rows + i * 32, 32), 32)
+                total = pl.ds(pl.multiple_of(tile * d, 128), d)
                 h = ps[0, at_rows, pl.ds(0, d)].astype(F32)
-                by_a = da[at_all, :].astype(BF).astype(F32)
+                by_a = big[at_rows, total].astype(BF).astype(F32)
                 scale = lax.rsqrt(jnp.mean(h * h, -1, keepdims=True) + 1e-6)
                 along = jnp.sum(by_a * h, -1, keepdims=True)
                 by_h = (by_a * scale - h * (scale * scale * scale * along * (1.0 / d))).astype(BF)
@@ -450,64 +501,95 @@
 
     def tick(k, _):
         computes = k < PIECES
+        layer = layer_of(k)
         gated = jnp.logical_and(computes, is_wide(k))
         downs = jnp.logical_and(computes, jnp.logical_not(is_wide(k)))
-        downs_1 = jnp.logical_and(downs, layer_of(k) == 1)
+        downs_1 = jnp.logical_and(downs, layer == 1)
 
         @pl.when(downs)
         def _():
-            tile_start(k, 0)
-            tile_start(k, 1)
+            tile_start(k, 0, 0)
+            tile_start(k, 1, 1)
 
         @pl.when(downs_1)
         def _():
             for which in range(2):
                 w_copy(which, 1, 2 * part_of(k)).start()
 
-        for point in range(POINTS):
-            service(k, point)
-
-            @pl.when(gated)
-            def _(point=point):
-                if point == 0:
+        def serve(point, points):
+            for one in points:
+
+                @pl.when(point == one)
+                def _(one=one):
+                    service(k, one)
+
+        def fronts(point, _):
+            serve(point, range(4))
+
+            @pl.when(jnp.logical_and(gated, layer == 1))
+            def _():
+                @pl.when(point == 0)
+                def _():
                     for which in range(3):
-                        w_copy(which, layer_of(k), chunk_of(k)).wait()
-                if point < 4:
-                    front_tile(k, point)
-                else:
-                    weight_part(point // 2 - 2, point % 2, k)
-                if point == 3:
-                    @pl.when(jnp.logical_and(k != CHUNKS - 1, k < PIECES - 1))
-                    def _():
-                        for which in range(3):
-                            w_copy(which, layer_of(k), chunk_of(k) + 1).start()
-
-                if point == POINTS - 1:
-
-                    @pl.when(layer_of(k) == 1)
-                    def _():
-                        p_copy(k, tiles - 2).wait()
-                        p_copy(k, tiles - 1).wait()
-                        for which in range(2):
-                            for tile in range(tiles):
-                                d_copy(which, chunk_of(k), tile, False).wait()
-
-            if point < 4:
-
-                @pl.when(downs)
-                def _(point=point):
-                    down_tile(k, 2 * point)
-                    down_tile(k, 2 * point + 1)
-
-            else:
+                        w_copy(which, 1, chunk_of(k)).wait()
+
+                front_tile(k, point)
+
+            @pl.when(jnp.logical_and(gated, layer == 0))
+            def _():
+                @pl.when(point == 0)
+                def _():
+                    w_copy(2, 0, chunk_of(k)).wait()
+
+                kept_tile(k, point)
+
+            @pl.when(downs)
+            def _():
+                for which in range(2):
+                    down_tile(k, which, 2 * point + which)
+
+            return 0
+
+        lax.fori_loop(0, 4, fronts, 0)
+
+        @pl.when(k < CHUNKS - 1)
+        def _():
+            for which in range(3):
+                w_copy(which, 1, chunk_of(k) + 1).start()
+
+        @pl.when(jnp.logical_and(k >= CHUNKS + 2 * PARTS, k < PIECES - 1))
+        def _():
+            w_copy(2, 0, chunk_of(k) + 1).start()
+
+        @pl.when(downs_1)
+        def _():
+            for tile in range(tiles):
+                for which in range(2):
+                    d_copy(which, 2 * part_of(k), tile, True).start()
+
+        def backs(side, _):
+            for which in range(2):
+                serve(4 + 2 * side + which, (4 + which, 6 + which))
+
+                @pl.when(gated)
+                def _(which=which):
+                    weight_part(side, which, k)
 
                 @pl.when(downs_1)
-                def _(point=point):
-                    if point == 4:
-                        for tile in range(tiles):
-                            for which in range(2):
-                                d_copy(which, 2 * part_of(k), tile, True).start()
-                    through_layer(point % 2, 2 * part_of(k) + point // 2 - 2, point < 6)
+                def _(which=which):
+                    through_layer(which, k, side)
+
+            return 0
+
+        lax.fori_loop(0, 2, backs, 0)
+
+        @pl.when(jnp.logical_and(gated, layer == 1))
+        def _():
+            for tile in range(tiles - 2, tiles):
+                p_copy(k, tile).wait()
+            for which in range(2):
+                for tile in range(tiles):
+                    d_copy(which, chunk_of(k), tile, False).wait()
 
         @pl.when(k == CHUNKS - 1)
         def _():
@@ -515,9 +597,11 @@
 
         @pl.when(k == CHUNKS + PARTS - 1)
         def _():
-            for which in range(3):
-                w_copy(which, 0, 0).start()
+            w_copy(2, 0, 0).start()
             through_norm()
+            for tile in range(2):
+                for which in range(2):
+                    gu_copy(which, 0, tile).start()
             turn(dh, dht)
             x_copy.wait()
             norm_all()
@@ -527,40 +611,40 @@
     lax.fori_loop(0, TICKS, tick, 0)
 
 
-def train_step(x, dy, h, p0, weights, ms, vs):
+def train_step(x, dy, h, p0, gate, up, weights, ms, vs):
     tokens, d = dy.shape
     ff = p0.shape[1]
     c, r, e = ff // CHUNKS, d // 32, d // PARTS
     rows = min(512, tokens // 4)
     any_ = pl.BlockSpec(memory_space=pl.ANY)
-    blocks = lambda *n: pltpu.VMEM((*n, r, e), BF)
+    blocks = lambda *n: pltpu.VMEM((*n, GROUPS, r, e), BF)
     scratch = [
         pltpu.VMEM((tokens, d), BF), pltpu.VMEM((d, tokens), BF), pltpu.VMEM((tokens, d), BF), pltpu.VMEM((d, tokens), BF),
         pltpu.VMEM((d, c), BF), pltpu.VMEM((d, c), BF), pltpu.VMEM((c, d), BF),
         pltpu.VMEM((tokens, c), BF), pltpu.VMEM((tokens, c), BF),
         pltpu.VMEM((2, rows, c), BF),
-        pltpu.VMEM((tokens, d), F32),
+        pltpu.VMEM((rows, 4 * c), F32),
         blocks(2, SUBS, 32), blocks(2, SUBS, 32),
         *[blocks(2, SUBS, 16 >> s) for s in range(STAGES)] * 2,
         *[blocks(SUBS, 16 >> s) for s in range(STAGES - 1)] * 2,
-        blocks(2, SUBS), pltpu.VMEM((2, SUBS, r, e), F32), pltpu.VMEM((2, SUBS, r, e), F32), blocks(2, SUBS),
+        blocks(2, SUBS), *[pltpu.VMEM((2, SUBS, GROUPS, r, e), F32)] * 2, blocks(2, SUBS),
         pltpu.SemaphoreType.DMA((2, STAGES, SUBS)), pltpu.SemaphoreType.DMA((2, STAGES, SUBS, 2)),
         pltpu.SemaphoreType.DMA((2, STAGES, SUBS)), pltpu.SemaphoreType.DMA((2, STAGES, SUBS, 2)),
         pltpu.SemaphoreType.DMA((2, SUBS)), pltpu.SemaphoreType.DMA((4,)), pltpu.SemaphoreType.DMA((3,)), pltpu.SemaphoreType.DMA((2,)),
-        pltpu.SemaphoreType.DMA((2, 3, SUBS)), pltpu.SemaphoreType.DMA((2, 4)),
+        pltpu.SemaphoreType.DMA((2, 3, 4)), pltpu.SemaphoreType.DMA((2, 4)), pltpu.SemaphoreType.DMA((4,)),
     ]
-    packed = jax.ShapeDtypeStruct((PIECES, SUBS, 32, r, e), BF)
+    packed = jax.ShapeDtypeStruct((PIECES, SUBS, 32, GROUPS, r, e), BF)
     like = [jax.ShapeDtypeStruct(t.shape, F32) for t in (*ms, *vs)]
     return pl.pallas_call(
         step_kernel,
         name="step",
-        in_specs=[any_] * 13,
+        in_specs=[any_] * 15,
         out_specs=[any_] * 11,
         out_shape=[packed, packed, *like, *[jax.ShapeDtypeStruct((tokens, ff), BF)] * 3],
         scratch_shapes=scratch,
         compiler_params=pltpu.CompilerParams(collective_id=0, has_side_effects=True, vmem_limit_bytes=67_000_000),
         cost_estimate=pl.CostEstimate(flops=28 * tokens * d * ff, bytes_accessed=400 << 20, transcendentals=0),
-    )(x, dy, h, p0, *weights, *ms, *vs)
+    )(x, dy, h, p0, gate, up, *weights, *ms, *vs)
 
 
 def unpack_kernel(gate_ref, up_ref, down_a, down_b, *refs):
@@ -572,27 +656,28 @@
         for z0 in range(2):
             for z1 in range(2):
                 owner = z1 * 4 + z0 * 2 + core
-                for sub in range(SUBS):
+                for group in range(4):
+                    sub, q = group // GROUPS, group % GROUPS
                     for chunk in range(CHUNKS):
-                        at_rows, at_cols = pl.ds(owner * r, r), pl.ds((chunk * SUBS + sub) * e, e)
-                        wg_ref[at_rows, at_cols] = gate_ref[chunk, sub, core, z0, z1]
-                        wu_ref[at_rows, at_cols] = up_ref[chunk, sub, core, z0, z1]
+                        at_rows, at_cols = pl.ds(owner * r, r), pl.ds((chunk * 4 + group) * e, e)
+                        wg_ref[at_rows, at_cols] = gate_ref[chunk, sub, core, z0, z1, q]
+                        wu_ref[at_rows, at_cols] = up_ref[chunk, sub, core, z0, z1, q]
                     for part in range(PARTS):
                         for half, ref in enumerate((down_a, down_b)):
-                            at_rows = pl.ds((owner * 8 + half * SUBS + sub) * r, r)
-                            wd_ref[at_rows, pl.ds(part * e, e)] = ref[part, sub, core, z0, z1]
+                            at_rows = pl.ds((owner * 8 + half * 4 + group) * r, r)
+                            wd_ref[at_rows, pl.ds(part * e, e)] = ref[part, sub, core, z0, z1, q]
 
 
 def unpack(wa, wb, moments, d, ff):
     r, e = wa.shape[-2:]
-    wa, wb = (t.reshape(PIECES, SUBS, *(2,) * 5, r, e) for t in (wa, wb))
+    wa, wb = (t.reshape(PIECES, SUBS, *(2,) * 5, GROUPS, r, e) for t in (wa, wb))
 
     def spec(n, first, half):
         def index(layer, x, y):
             outer, inner = (x, y) if half == 0 else (y, x)
-            return (first(layer), 0, 0, outer, 0, inner, 0, 0, 0)
-
-        return pl.BlockSpec((n, SUBS, 2, None, 2, None, 2, r, e), index)
+            return (first(layer), 0, 0, outer, 0, inner, 0, 0, 0, 0)
+
+        return pl.BlockSpec((n, SUBS, 2, None, 2, None, 2, GROUPS, r, e), index)
 
     wide, part = lambda layer: 2 - 2 * layer, lambda layer: 3 - layer
     slab = lambda rows, cols: pl.BlockSpec((None, rows, cols), lambda layer, x, y: (layer, 2 * x + y, 0))
@@ -617,8 +702,8 @@
         wg, wu, wd = arrays[:3]
         ms, vs = arrays[3:6], arrays[6:9]
         x, dy = x[0], dy[0]
-        p0, h = forward(x, wg, wu, wd, 0)
-        wa, wb, *moments, _, _, _ = train_step(x, dy, h, p0, (wg, wu, wd), ms, vs)
+        p0, h, gate, up = forward(x, wg, wu, wd, 0)
+        wa, wb, *moments, _, _, _ = train_step(x, dy, h, p0, gate, up, (wg, wu, wd), ms, vs)
         return tuple(unpack(wa, wb, moments, x.shape[1], wg.shape[2]))
 
     seq, whole, rows = P(("rep", "dp")), P(), P(None, "dp")

time: 653 us -> 653 us (level)
    pallas_call x1, Pallas kernels: 534 us -> 521 us  [train_step(): pl.pallas_call(step_kernel, name='step', in_specs=[any_] * 15, out_specs=...]
    pallas_call x1, Pallas kernels: 76.3 us -> 89.2 us  [forward(): pl.pallas_call(forward_kernel, name='forward', grid=(CHUNKS, tokens // ro...]
where the time goes in v5:
time: 653 us; the launch traced here: 652 us
  Pallas kernels  651 us (100%)
    pallas_call x1, Pallas kernels, train_step(): pl.pallas_call(step_kernel, name='step', in_specs=[any_] * 15, out_specs=...  521 us
    pallas_call x1, Pallas kernels, forward(): pl.pallas_call(forward_kernel, name='forward', grid=(CHUNKS, tokens // ro...  89.2 us
    pallas_call x1, Pallas kernels, unpack(): pl.pallas_call(unpack_kernel, name='unpack', grid=(2, 2, 2), in_specs=[sp...  40.7 us

profile of v5, /device:TPU:0, one launch (start us, length us, event | category | flops | bytes accessed | tf_op | source)
XLA Modules:
  0.0 651.7 jit_solution(13803286498052728128)
XLA Ops:
  0.6 89.2 %forward.1 = (bf16[2048,6144]{1,0:T(8,128)(2,1)}, bf16[2048,768]{1,0:T(8,128)(2,1)}, f32[2048,6144]{1,0:T(8,128)}, f32[2048,6144]{1,0:T(8,128)}) custom-call(bf16[2048,768]{1,0:T(8,128)(2,1)} %bitcast.8, bf16[2,768,6144]{2,1,0:T(8,128)(2,1)} %wg_hbm.1, bf16[2,768,6144]{2,1,0:T(8,128)(2,1)} %wu_hbm.1, bf16[2,6144,768]{2,1,0:T(8,128)(2,1)} %wd_hbm.1), custom_call_target="tpu_custom_call" | custom-call | flops 57982058496 | bytes 62914560 | tf_op jit(solution)/shard_map/forward/pallas_call | solution.py:97
  89.8 521.0 %step.1 = (bf16[18,2,32,2,24,256]{5,4,3,2,1,0:T(8,128)(2,1)}, bf16[18,2,32,2,24,256]{5,4,3,2,1,0:T(8,128)(2,1)}, f32[2,24,6144]{2,1,0:T(8,128)}, f32[2,24,6144]{...) custom-call(bf16[2048,768]{1,0:T(8,128)(2,1)} %bitcast.9, ...), custom_call_target="tpu_custom_call" | custom-call | flops 270582939648 | bytes 419430400 | tf_op jit(solution)/shard_map/step/pallas_call | solution.py:638
  610.9 40.7 %unpack.1 = (bf16[2,768,6144]{2,1,0:T(8,128)(2,1)}, bf16[2,768,6144]{2,1,0:T(8,128)(2,1)}, bf16[2,6144,768]{2,1,0:T(8,128)(2,1)}, f32[2,24,6144]{2,1,0:T(8,128)}...) custom-call(bf16[18,2,2,2,2,2,2,2,24,256]{9,8,7,6,5,4,3,2,1,0:T(8,12, ...), custom_call_target="tpu_custom_call" | custom-call | tf_op jit(solution)/shard_map/unpack/pallas_call | solution.py:687

commit v6 on v5

--- a/solution.py
+++ b/solution.py
@@ -24,8 +24,8 @@
 GROUPS = 4 // SUBS
 POINTS = 8
 TIMES = (
-    (8, 9, 13, 17, 20, 24, 28, 31, 38, 44, 48),
-    (10, 11, 15, 21, 23, 26, 31, 35, 40, 47, 55),
+    (8, 9, 12, 17, 20, 24, 28, 30, 37, 41, 45),
+    (9, 10, 14, 20, 22, 26, 29, 34, 39, 47, 51),
 )
 TICKS = PIECES + max(t[-1] for t in TIMES) // POINTS
 
@@ -68,7 +68,7 @@
 
     @pl.when(chunk == 0)
     def _():
-        a_all[here, :] = normed(x_ref[here, :])
+        a_all[here, :] = normed(x_ref[...])
 
     a = a_all[here, :]
     gate, up = dot(a, wg_ref[...]), dot(a, wu_ref[...])
@@ -87,32 +87,33 @@
     @pl.when(chunk == pl.num_programs(0) - 1)
     def _():
         down = total[here, :].astype(BF).astype(F32)
-        h_ref[here, :] = (x_ref[here, :].astype(F32) + down).astype(BF)
+        h_ref[...] = (x_ref[...].astype(F32) + down).astype(BF)
 
 
 def forward(x, wg, wu, wd, layer):
     tokens, d = x.shape
     ff = wg.shape[-1]
-    c, rows = ff // CHUNKS, min(512, tokens)
+    c, rows = ff // CHUNKS, min(512, tokens // 4)
+    last = tokens // rows - 1
     return pl.pallas_call(
         forward_kernel,
         name="forward",
         grid=(CHUNKS, tokens // rows),
         in_specs=[
-            pl.BlockSpec((tokens, d), lambda i, t: (0, 0)),
+            pl.BlockSpec((rows, d), lambda i, t: (jnp.where((i == 0) | (i == CHUNKS - 1), t, last), 0)),
             pl.BlockSpec((None, d, c), lambda i, t: (layer, 0, i)),
             pl.BlockSpec((None, d, c), lambda i, t: (layer, 0, i)),
             pl.BlockSpec((None, c, d), lambda i, t: (layer, i, 0)),
         ],
         out_specs=[
             pl.BlockSpec((rows, c), lambda i, t: (t, i)),
-            pl.BlockSpec((tokens, d), lambda i, t: (0, 0)),
-            *[pl.BlockSpec((rows, c), lambda i, t: (t, i))] * 2,
+            pl.BlockSpec((rows, d), lambda i, t: (jnp.where(i == CHUNKS - 1, t, 0), 0)),
+            *[pl.BlockSpec((None, rows, c), lambda i, t: (i, t, 0))] * 2,
         ],
         out_shape=[
             jax.ShapeDtypeStruct((tokens, ff), BF),
             jax.ShapeDtypeStruct((tokens, d), BF),
-            *[jax.ShapeDtypeStruct((tokens, ff), F32)] * 2,
+            *[jax.ShapeDtypeStruct((CHUNKS, tokens, c), F32)] * 2,
         ],
         scratch_shapes=[pltpu.VMEM((tokens, d), BF), pltpu.VMEM((tokens, d), F32)],
         compiler_params=pltpu.CompilerParams(vmem_limit_bytes=60 << 20),
@@ -324,7 +325,7 @@
 
     def d_copy(which, chunk, tile, load):
         here = pl.ds(pl.multiple_of(tile * rows, rows), rows)
-        vmem, hbm = (dg, du)[which].at[here, :], (dg_hbm, du_hbm)[which].at[here, pl.ds(pl.multiple_of(chunk * c, c), c)]
+        vmem, hbm = (dg, du)[which].at[here, :], (dg_hbm, du_hbm)[which].at[chunk, here, :]
         return pltpu.make_async_copy(*((hbm, vmem) if load else (vmem, hbm)), d_sem.at[which, tile])
 
     def front_tile(piece, tile):
@@ -356,8 +357,8 @@
 
     def gu_copy(which, chunk, tile):
         slot = 2 * (tile % 2) + which
-        source = (gate_hbm, up_hbm)[which].at[pl.ds(pl.multiple_of(tile * rows, rows), rows), pl.ds(pl.multiple_of(chunk * c, c), c)]
-        return pltpu.make_async_copy(source, big.at[:, pl.ds(pl.multiple_of(slot * c, c), c)], gu_sem.at[slot])
+        source = (gate_hbm, up_hbm)[which].at[chunk, pl.ds(pl.multiple_of(tile * rows, rows), rows), :]
+        return pltpu.make_async_copy(source, big.at[slot], gu_sem.at[slot])
 
     def kept_tile(piece, tile):
         here = pl.ds(pl.multiple_of(tile * rows, rows), rows)
@@ -368,9 +369,9 @@
         for j in range(FRONT):
             cols = slice(j * n, (j + 1) * n)
             dps = dot(dh_, wd[cols, :], NT)
-            at_gate, at_up = (pl.ds(pl.multiple_of((2 * (tile % 2) + which) * c + j * n, n), n) for which in range(2))
+            slot = 2 * (tile % 2)
             for i in range(0, rows, STRIP):
-                gate, up = big[i : i + STRIP, at_gate], big[i : i + STRIP, at_up]
+                gate, up = big[slot, i : i + STRIP, cols], big[slot + 1, i : i + STRIP, cols]
                 dp = dps[i : i + STRIP].astype(BF).astype(F32)
                 s = sigmoid(gate)
                 gs = gate * s
@@ -400,13 +401,13 @@
 
         def back(tile, _):
             here = pl.ds(pl.multiple_of(tile * rows, rows), rows)
-            total = pl.ds(pl.multiple_of(tile * d, 128), d)
+            total = pl.ds(0, d)
             d_copy(which, chunk, tile, True).wait()
             part = dot((dg, du)[which][here, :], (wg, wu)[which][...], NT)
             if which == 0:
-                big[:, total] = jnp.where(chunk == 0, jnp.zeros_like(part), big[:, total]) + part
+                big[tile, :, total] = jnp.where(chunk == 0, jnp.zeros_like(part), big[tile, :, total]) + part
             else:
-                big[:, total] += part
+                big[tile, :, total] += part
 
             @pl.when(side == 0)
             def _():
@@ -445,19 +446,19 @@
         def _():
             tile_start(piece, which, tile + 2)
 
+    def h_copy(tile):
+        slot, here = tile % 2, pl.ds(pl.multiple_of(tile * rows, rows), rows)
+        return pltpu.make_async_copy(h_hbm.at[here, :], ps.at[slot, :, pl.ds(0, d)], p_sem.at[slot])
+
     def through_norm():
         def back(tile, _):
-            here = pl.ds(pl.multiple_of(tile * rows, rows), rows)
-            load = pltpu.make_async_copy(h_hbm.at[here, :], ps.at[0, :, pl.ds(0, d)], p_sem.at[0])
-            load.start()
-            load.wait()
+            h_copy(tile).wait()
 
             def some(i, _):
                 at_rows = pl.ds(pl.multiple_of(i * 32, 32), 32)
                 at_all = pl.ds(pl.multiple_of(tile * rows + i * 32, 32), 32)
-                total = pl.ds(pl.multiple_of(tile * d, 128), d)
-                h = ps[0, at_rows, pl.ds(0, d)].astype(F32)
-                by_a = big[at_rows, total].astype(BF).astype(F32)
+                h = ps[tile % 2, at_rows, pl.ds(0, d)].astype(F32)
+                by_a = big[tile, at_rows, pl.ds(0, d)].astype(BF).astype(F32)
                 scale = lax.rsqrt(jnp.mean(h * h, -1, keepdims=True) + 1e-6)
                 along = jnp.sum(by_a * h, -1, keepdims=True)
                 by_h = (by_a * scale - h * (scale * scale * scale * along * (1.0 / d))).astype(BF)
@@ -465,6 +466,11 @@
                 return 0
 
             lax.fori_loop(0, rows // 32, some, 0)
+
+            @pl.when(tile + 2 < tiles)
+            def _():
+                h_copy(tile + 2).start()
+
             return 0
 
         lax.fori_loop(0, tiles, back, 0)
@@ -594,6 +600,8 @@
         @pl.when(k == CHUNKS - 1)
         def _():
             x_copy.start()
+            for tile in range(2):
+                h_copy(tile).start()
 
         @pl.when(k == CHUNKS + PARTS - 1)
         def _():
@@ -603,6 +611,9 @@
                 for which in range(2):
                     gu_copy(which, 0, tile).start()
             turn(dh, dht)
+
+        @pl.when(k == CHUNKS + PARTS)
+        def _():
             x_copy.wait()
             norm_all()
 
@@ -623,7 +634,7 @@
         pltpu.VMEM((d, c), BF), pltpu.VMEM((d, c), BF), pltpu.VMEM((c, d), BF),
         pltpu.VMEM((tokens, c), BF), pltpu.VMEM((tokens, c), BF),
         pltpu.VMEM((2, rows, c), BF),
-        pltpu.VMEM((rows, 4 * c), F32),
+        pltpu.VMEM((4, rows, c), F32),
         blocks(2, SUBS, 32), blocks(2, SUBS, 32),
         *[blocks(2, SUBS, 16 >> s) for s in range(STAGES)] * 2,
         *[blocks(SUBS, 16 >> s) for s in range(STAGES - 1)] * 2,
@@ -640,7 +651,7 @@
         name="step",
         in_specs=[any_] * 15,
         out_specs=[any_] * 11,
-        out_shape=[packed, packed, *like, *[jax.ShapeDtypeStruct((tokens, ff), BF)] * 3],
+        out_shape=[packed, packed, *like, jax.ShapeDtypeStruct((tokens, ff), BF), *[jax.ShapeDtypeStruct((CHUNKS, tokens, c), BF)] * 2],
         scratch_shapes=scratch,
         compiler_params=pltpu.CompilerParams(collective_id=0, has_side_effects=True, vmem_limit_bytes=67_000_000),
         cost_estimate=pl.CostEstimate(flops=28 * tokens * d * ff, bytes_accessed=400 << 20, transcendentals=0),

time: 653 us -> 646 us (0.989)
  no operation moved by 1% of the time
where the time goes in v6:
time: 646 us
  Pallas kernels  645 us (100%)
    pallas_call x1, Pallas kernels, train_step(): pl.pallas_call(step_kernel, name='step', in_specs=[any_] * 15, out_specs=...  516 us
    pallas_call x1, Pallas kernels, forward(): pl.pallas_call(forward_kernel, name='forward', grid=(CHUNKS, tokens // ro...  88.6 us
    pallas_call x1, Pallas kernels, unpack(): pl.pallas_call(unpack_kernel, name='unpack', grid=(2, 2, 2), in_specs=[sp...  40.7 us

profile of v6, /device:TPU:0, one launch (start us, length us, event | category | flops | bytes accessed | tf_op | source)
XLA Modules:
  0.0 645.6 jit_solution(4594046896198802560)
XLA Ops:
  0.6 88.6 %forward.1 = (bf16[2048,6144]{1,0:T(8,128)(2,1)}, bf16[2048,768]{1,0:T(8,128)(2,1)}, f32[6,2048,1024]{2,1,0:T(8,128)}, f32[6,2048,1024]{2,1,0:T(8,128)}) custom-call(bf16[2048,768]{1,0:T(8,128)(2,1)} %bitcast.8, bf16[2,768,6144]{2,1,0:T(8,128)(2,1)} %wg_hbm.1, bf16[2,768,6144]{2,1,0:T(8,128)(2,1)} %wu_hbm.1, bf16[2,6144,768]{2,1,0:T(8,128)(2,1)} %wd_hbm.1), custom_call_target="tpu_custom_call" | custom-call | flops 57982058496 | bytes 62914560 | tf_op jit(solution)/shard_map/forward/pallas_call | solution.py:98
  89.2 515.5 %step.1 = (bf16[18,2,32,2,24,256]{5,4,3,2,1,0:T(8,128)(2,1)}, bf16[18,2,32,2,24,256]{5,4,3,2,1,0:T(8,128)(2,1)}, f32[2,24,6144]{2,1,0:T(8,128)}, f32[2,24,6144]{...) custom-call(bf16[2048,768]{1,0:T(8,128)(2,1)} %bitcast.9, ...), custom_call_target="tpu_custom_call" | custom-call | flops 270582939648 | bytes 419430400 | tf_op jit(solution)/shard_map/step/pallas_call | solution.py:649
  604.8 40.7 %unpack.1 = (bf16[2,768,6144]{2,1,0:T(8,128)(2,1)}, bf16[2,768,6144]{2,1,0:T(8,128)(2,1)}, bf16[2,6144,768]{2,1,0:T(8,128)(2,1)}, f32[2,24,6144]{2,1,0:T(8,128)}...) custom-call(bf16[18,2,2,2,2,2,2,2,24,256]{9,8,7,6,5,4,3,2,1,0:T(8,12, ...), custom_call_target="tpu_custom_call" | custom-call | tf_op jit(solution)/shard_map/unpack/pallas_call | solution.py:698

commit v7 on v6

--- a/solution.py
+++ b/solution.py
@@ -19,13 +19,14 @@
 PARTS = 3
 PIECES = 2 * (CHUNKS + PARTS)
 FRONT = 4
-STRIP = 32
+STRIP = 128
 SUBS = 2
 GROUPS = 4 // SUBS
+SLOTS = 4
 POINTS = 8
 TIMES = (
-    (8, 9, 12, 17, 20, 24, 28, 30, 37, 41, 45),
-    (9, 10, 14, 20, 22, 26, 29, 34, 39, 47, 51),
+    (8, 9, 13, 17, 21, 24, 28, 31, 38, 42, 45),
+    (10, 11, 16, 21, 23, 27, 31, 35, 40, 48, 53),
 )
 TICKS = PIECES + max(t[-1] for t in TIMES) // POINTS
 
@@ -150,7 +151,7 @@
     def rs_copy(half, stage, piece, sub):
         bit = ORDERS[half][stage]
         own, n = bit_of(me, bit), 16 >> stage
-        source = g_bufs[half].at[piece % 2, sub] if stage == 0 else s_bufs[half][stage - 1].at[sub]
+        source = g_bufs[half].at[piece % SLOTS, sub] if stage == 0 else s_bufs[half][stage - 1].at[sub]
         return pltpu.make_async_remote_copy(
             src_ref=source.at[pl.ds((1 - own) * n, n)],
             dst_ref=r_bufs[half][stage].at[piece % 2, sub],
@@ -175,7 +176,7 @@
         some = min(n, SUBS)
         for half in range(2):
             own = bit_of(me, ORDERS[half][stage])
-            source = g_bufs[half].at[piece % 2, sub] if stage == 0 else s_bufs[half][stage - 1].at[sub]
+            source = g_bufs[half].at[piece % SLOTS, sub] if stage == 0 else s_bufs[half][stage - 1].at[sub]
             got, to = r_bufs[half][stage].at[piece % 2, sub], s_bufs[half][stage].at[sub]
 
             def add(i, _, source=source, got=got, to=to, own=own):
@@ -388,15 +389,15 @@
 
     def weight_part(side, which, piece):
         n = c // 2
+        slot = piece % SLOTS
         term = dot(at[...], (dg, du)[which][:, pl.ds(pl.multiple_of(side * n, n), n)])
         for i in range(32):
             for q in range(2):
                 group = side * 2 + q
                 block = term[i * r : (i + 1) * r, q * e : (q + 1) * e].astype(BF)
-                (ga, gb)[which][piece % 2, group // GROUPS, place(i, ORDERS[which]), group % GROUPS] = block
-
-    def through_layer(which, piece, side):
-        chunk = 2 * part_of(piece) + side
+                (ga, gb)[which][slot, group // GROUPS, place(i, ORDERS[which]), group % GROUPS] = block
+
+    def through_layer(which, chunk, more):
         w_copy(which, 1, chunk).wait()
 
         def back(tile, _):
@@ -409,7 +410,7 @@
             else:
                 big[tile, :, total] += part
 
-            @pl.when(side == 0)
+            @pl.when(more)
             def _():
                 d_copy(which, chunk + 1, tile, True).start()
 
@@ -417,7 +418,7 @@
 
         lax.fori_loop(0, tiles, back, 0)
 
-        @pl.when(side == 0)
+        @pl.when(more)
         def _():
             w_copy(which, 1, chunk + 1).start()
 
@@ -432,15 +433,33 @@
             def _(source=source):
                 tile_copy(which, tile, source).start()
 
+    def down_all_tile(piece, which, tile):
+        tile_copy(which, tile, p0_hbm).wait()
+        places = [[place(4 * tile + i, order) for order in ORDERS] for i in range(4)]
+        slots = [(piece + part) % SLOTS for part in range(PARTS)]
+        for part in range(PARTS):
+            term = dot(dht[part * e : (part + 1) * e, :], (dg, du)[which][:, :wide]).T
+            for i in range(4):
+                for j in range(8):
+                    half, group = j // 4, j % 4
+                    block = term[(8 * i + j) * r : (8 * i + j + 1) * r, :].astype(BF)
+                    g_bufs[half][slots[part], group // GROUPS, places[i][half], group % GROUPS] = block
+
+        @pl.when(tile + 2 < 8)
+        def _():
+            tile_start(piece, which, tile + 2)
+
     def down_tile(piece, which, tile):
         tile_copy(which, tile, p0_hbm).wait()
         at_rows = pl.ds(pl.multiple_of(part_of(piece) * e, e), e)
+        places = [[place(4 * tile + i, order) for order in ORDERS] for i in range(4)]
+        slot = piece % SLOTS
         term = dot(dht[at_rows, :], (dg, du)[which][:, :wide]).T
         for i in range(4):
             for j in range(8):
                 half, group = j // 4, j % 4
                 block = term[(8 * i + j) * r : (8 * i + j + 1) * r, :].astype(BF)
-                g_bufs[half][piece % 2, group // GROUPS, place(4 * tile + i, ORDERS[half]), group % GROUPS] = block
+                g_bufs[half][slot, group // GROUPS, places[i][half], group % GROUPS] = block
 
         @pl.when(tile + 2 < 8)
         def _():
@@ -510,17 +529,22 @@
         layer = layer_of(k)
         gated = jnp.logical_and(computes, is_wide(k))
         downs = jnp.logical_and(computes, jnp.logical_not(is_wide(k)))
-        downs_1 = jnp.logical_and(downs, layer == 1)
-
-        @pl.when(downs)
+        downs_0 = jnp.logical_and(downs, layer == 0)
+        downs_1 = k == CHUNKS
+        through = jnp.logical_and(k > CHUNKS, k < CHUNKS + PARTS)
+        chunk = PARTS * (k - CHUNKS - 1)
+
+        @pl.when(jnp.logical_or(downs_0, downs_1))
         def _():
             tile_start(k, 0, 0)
             tile_start(k, 1, 1)
 
-        @pl.when(downs_1)
+        @pl.when(through)
         def _():
             for which in range(2):
-                w_copy(which, 1, 2 * part_of(k)).start()
+                w_copy(which, 1, chunk).start()
+                for tile in range(tiles):
+                    d_copy(which, chunk, tile, True).start()
 
         def serve(point, points):
             for one in points:
@@ -549,11 +573,22 @@
 
                 kept_tile(k, point)
 
-            @pl.when(downs)
+            @pl.when(downs_0)
             def _():
                 for which in range(2):
                     down_tile(k, which, 2 * point + which)
 
+            @pl.when(downs_1)
+            def _():
+                for which in range(2):
+                    down_all_tile(k, which, 2 * point + which)
+
+            for which in range(2):
+
+                @pl.when(jnp.logical_and(through, point == 2 * which))
+                def _(which=which):
+                    through_layer(which, chunk, True)
+
             return 0
 
         lax.fori_loop(0, 4, fronts, 0)
@@ -566,12 +601,6 @@
         @pl.when(jnp.logical_and(k >= CHUNKS + 2 * PARTS, k < PIECES - 1))
         def _():
             w_copy(2, 0, chunk_of(k) + 1).start()
-
-        @pl.when(downs_1)
-        def _():
-            for tile in range(tiles):
-                for which in range(2):
-                    d_copy(which, 2 * part_of(k), tile, True).start()
 
         def backs(side, _):
             for which in range(2):
@@ -581,9 +610,9 @@
                 def _(which=which):
                     weight_part(side, which, k)
 
-                @pl.when(downs_1)
+                @pl.when(through)
                 def _(which=which):
-                    through_layer(which, k, side)
+                    through_layer(which, chunk + 1 + side, side == 0)
 
             return 0
 
@@ -635,7 +664,7 @@
         pltpu.VMEM((tokens, c), BF), pltpu.VMEM((tokens, c), BF),
         pltpu.VMEM((2, rows, c), BF),
         pltpu.VMEM((4, rows, c), F32),
-        blocks(2, SUBS, 32), blocks(2, SUBS, 32),
+        blocks(SLOTS, SUBS, 32), blocks(SLOTS, SUBS, 32),
         *[blocks(2, SUBS, 16 >> s) for s in range(STAGES)] * 2,
         *[blocks(SUBS, 16 >> s) for s in range(STAGES - 1)] * 2,
         blocks(2, SUBS), *[pltpu.VMEM((2, SUBS, GROUPS, r, e), F32)] * 2, blocks(2, SUBS),

time: 646 us -> 640 us (level)
  no operation moved by 1% of the time
where the time goes in v7:
time: 640 us
  Pallas kernels  639 us (100%)
    pallas_call x1, Pallas kernels, train_step(): pl.pallas_call(step_kernel, name='step', in_specs=[any_] * 15, out_specs=...  510 us
    pallas_call x1, Pallas kernels, forward(): pl.pallas_call(forward_kernel, name='forward', grid=(CHUNKS, tokens // ro...  88.6 us
    pallas_call x1, Pallas kernels, unpack(): pl.pallas_call(unpack_kernel, name='unpack', grid=(2, 2, 2), in_specs=[sp...  40.7 us

profile of v7, /device:TPU:0, one launch (start us, length us, event | category | flops | bytes accessed | tf_op | source)
XLA Modules:
  0.0 639.6 jit_solution(17267809989950214109)
XLA Ops:
  0.6 88.6 %forward.1 = (bf16[2048,6144]{1,0:T(8,128)(2,1)}, bf16[2048,768]{1,0:T(8,128)(2,1)}, f32[6,2048,1024]{2,1,0:T(8,128)}, f32[6,2048,1024]{2,1,0:T(8,128)}) custom-call(bf16[2048,768]{1,0:T(8,128)(2,1)} %bitcast.8, bf16[2,768,6144]{2,1,0:T(8,128)(2,1)} %wg_hbm.1, bf16[2,768,6144]{2,1,0:T(8,128)(2,1)} %wu_hbm.1, bf16[2,6144,768]{2,1,0:T(8,128)(2,1)} %wd_hbm.1), custom_call_target="tpu_custom_call" | custom-call | flops 57982058496 | bytes 62914560 | tf_op jit(solution)/shard_map/forward/pallas_call | solution.py:99
  89.2 509.6 %step.1 = (bf16[18,2,32,2,24,256]{5,4,3,2,1,0:T(8,128)(2,1)}, bf16[18,2,32,2,24,256]{5,4,3,2,1,0:T(8,128)(2,1)}, f32[2,24,6144]{2,1,0:T(8,128)}, f32[2,24,6144]{...) custom-call(bf16[2048,768]{1,0:T(8,128)(2,1)} %bitcast.9, ...), custom_call_target="tpu_custom_call" | custom-call | flops 270582939648 | bytes 419430400 | tf_op jit(solution)/shard_map/step/pallas_call | solution.py:678
  598.8 40.7 %unpack.1 = (bf16[2,768,6144]{2,1,0:T(8,128)(2,1)}, bf16[2,768,6144]{2,1,0:T(8,128)(2,1)}, bf16[2,6144,768]{2,1,0:T(8,128)(2,1)}, f32[2,24,6144]{2,1,0:T(8,128)}...) custom-call(bf16[18,2,2,2,2,2,2,2,24,256]{9,8,7,6,5,4,3,2,1,0:T(8,12, ...), custom_call_target="tpu_custom_call" | custom-call | tf_op jit(solution)/shard_map/unpack/pallas_call | solution.py:727
